TPU v7x, 256 devices: a whole 4x4x8 slice. The times are simulated.
256 devices in a mesh: dap: 16 (over x, z_lo), cplx: 16 (over y, z_hi, core).
Axes of the slice: x: 4, y: 4, z: 8 (z_hi: 2, z_lo: 4; z = z_hi * 4 + z_lo), core: 2. Of those that a mesh axis runs over, the one named last changes fastest.
Arguments:
- pair: bfloat16 [192, 3072, 128], P('dap', 'cplx'), parts along dimension 1, may hold values from -6 to 6
- cotangent: bfloat16 [192, 3072, 128], P('dap', 'cplx'), parts along dimension 1, may hold values from -6 to 6
- residue_mask: int32 [3072], P('cplx'), parts along dimension 0, may hold values 0 or 1
- chain_ids: int32 [3072], P('cplx'), parts along dimension 0, may hold values from 0 to 2, never falling along the last dimension, each value on 1 to 96 neighbouring positions
- chain_embed: float32 [2, 128], replicated, may hold values from -4 to 4
- out_norm_gain: float32 [128], replicated, may hold values from 0.25 to 1.75
- out_proj: bfloat16 [128, 512], replicated, may hold values from -0.5 to 0.5
- out_gate: bfloat16 [128, 128], replicated, may hold values from -0.5 to 0.5
- out_mid_gain: float32 [128], replicated, may hold values from 0.25 to 1.75
- out_final: bfloat16 [128, 128], replicated, may hold values from -0.5 to 0.5
- in_norm_gain: float32 [128], replicated, may hold values from 0.25 to 1.75
- in_proj: bfloat16 [128, 512], replicated, may hold values from -0.5 to 0.5
- in_gate: bfloat16 [128, 128], replicated, may hold values from -0.5 to 0.5
- in_mid_gain: float32 [128], replicated, may hold values from 0.25 to 1.75
- in_final: bfloat16 [128, 128], replicated, may hold values from -0.5 to 0.5
Outputs:
- pair_grad: bfloat16 [192, 3072, 128], P('dap', 'cplx'), parts along dimension 1
- grad_proj: float32 [2048, 512], P('cplx'), parts along dimension 0
- grad_gate: float32 [2048, 128], P('cplx'), parts along dimension 0
- grad_final: float32 [2048, 128], P('cplx'), parts along dimension 0
- grad_norm_gain: float32 [2048], P('cplx'), parts along dimension 0
- grad_mid_gain: float32 [2048], P('cplx'), parts along dimension 0
There are 16 independent parts, one for each index of `cplx`. A program takes and returns all parts, laid end to end along the dimension named above; an argument that names none is the same for every part. Nothing has to cross between parts.
Inputs may be any that keep to these rules, and one draw needn't show every extreme that they name: `chain_ids`: chain numbers never fall along the residues; each chain has at most 96 residues.
All inputs are finite; a program needn't handle non-finite values.
Results may differ from a plain program's by a relative error of at most 0.019.
Values may be sent and summed in bfloat16 or wider, within the bound.
A program may use at most 128 MiB of HBM per device.

v0:
```python
import jax
import jax.numpy as jnp
from jax import lax
from jax.sharding import PartitionSpec as P


def together(arrays, axis):
    ends = [0]
    for a in arrays:
        ends.append(ends[-1] + a.size)
    subtotal = lax.psum(jnp.concatenate([a.ravel() for a in arrays]), axis)
    return tuple((subtotal[b:e].reshape(a.shape) for a, b, e in zip(arrays, ends, ends[1:])))


def layer_norm(values_in, gain):
    average = jnp.mean(values_in, axis=-1, keepdims=True)
    centred = values_in - average
    variance = jnp.mean(centred * centred, axis=-1, keepdims=True)
    return centred * lax.rsqrt(variance + 1e-05) * gain


def gated_pair(projected, pair_mask, hidden_width):
    masked = pair_mask[..., None]
    left_act = (
        masked
        * jax.nn.sigmoid(projected[..., :hidden_width])
        * projected[..., hidden_width : 2 * hidden_width]
    )
    right_act = (
        masked
        * jax.nn.sigmoid(projected[..., 2 * hidden_width : 3 * hidden_width])
        * projected[..., 3 * hidden_width :]
    )
    return (left_act, right_act)


def shards(
    pair,
    cotangent,
    residue_mask,
    chain_ids,
    chain_embed,
    out_norm_gain,
    out_proj,
    out_gate,
    out_mid_gain,
    out_final,
    in_norm_gain,
    in_proj,
    in_gate,
    in_mid_gain,
    in_final,
):
    f32 = jnp.float32
    bf16 = jnp.bfloat16
    row_count = pair.shape[0]
    res_count = pair.shape[1]
    hidden_width = out_final.shape[0]
    inv_count = 1.0 / res_count
    row_start = lax.axis_index("dap") * row_count
    row_mask = lax.dynamic_slice_in_dim(residue_mask, row_start, row_count, 0)
    row_chain = lax.dynamic_slice_in_dim(chain_ids, row_start, row_count, 0)
    pair_mask = (row_mask[:, None] * residue_mask[None, :]).astype(f32)
    same_chain = row_chain[:, None] == chain_ids[None, :]
    start = pair.astype(f32) + jnp.where(same_chain[..., None], chain_embed[1], chain_embed[0])
    out_normed = layer_norm(start, out_norm_gain).astype(bf16)
    projected = jnp.dot(out_normed, out_proj, preferred_element_type=f32)
    left_act, right_act = gated_pair(projected, pair_mask, hidden_width)
    left_b = left_act.astype(bf16)
    right_b = right_act.astype(bf16)
    x_out = jnp.einsum(
        "ikc,jkc->ijc",
        left_b,
        lax.all_gather(right_b, "dap", axis=0, tiled=True),
        preferred_element_type=f32,
    )
    y_out = layer_norm(x_out, out_mid_gain).astype(bf16)
    update = jax.nn.sigmoid(jnp.dot(out_normed, out_gate, preferred_element_type=f32)) * jnp.dot(
        y_out, out_final, preferred_element_type=f32
    )
    pair_mid = (start + update).astype(bf16)
    mid_f32 = pair_mid.astype(f32)
    normed_f32, norm_back = jax.vjp(layer_norm, mid_f32, in_norm_gain)
    in_normed = normed_f32.astype(bf16)
    proj_in = jnp.dot(in_normed, in_proj, preferred_element_type=f32)
    (left_in, right_in), glu_back = jax.vjp(
        lambda proj_val: gated_pair(proj_val, pair_mask, hidden_width), proj_in
    )
    left_ib = left_in.astype(bf16)
    right_ib = right_in.astype(bf16)
    columns = lax.all_to_all(left_ib, "dap", split_axis=1, concat_axis=0, tiled=True)
    left_block = columns
    x_in = jnp.einsum(
        "kic,kjc->ijc",
        left_block,
        lax.all_gather(right_ib, "dap", axis=0, tiled=True),
        preferred_element_type=f32,
    )
    y_f32, mid_back = jax.vjp(layer_norm, x_in, in_mid_gain)
    y_in = y_f32.astype(bf16)
    logit = jnp.dot(in_normed, in_gate, preferred_element_type=f32)
    value = jnp.dot(y_in, in_final, preferred_element_type=f32)
    sigma = jax.nn.sigmoid(logit)
    upstream = cotangent.astype(f32)
    grad_value = (upstream * sigma).astype(bf16)
    grad_logit = (upstream * value * sigma * (1.0 - sigma)).astype(bf16)
    grad_final = jnp.einsum("ijc,ijd->cd", y_in, grad_value, preferred_element_type=f32) * inv_count
    grad_gate = (
        jnp.einsum("ijc,ijd->cd", in_normed, grad_logit, preferred_element_type=f32) * inv_count
    )
    grad_y = jnp.dot(grad_value, in_final.T, preferred_element_type=f32)
    grad_x, grad_mid = mid_back(grad_y)
    grad_x_b = grad_x.astype(bf16)
    shard_rows = lax.all_gather(grad_x_b, "dap", axis=0, tiled=True)
    left_block = left_ib
    grad_right = jnp.einsum("kic,ijc->kjc", left_block, shard_rows, preferred_element_type=f32)
    new_block = jnp.einsum("kjc,ijc->kic", right_ib, shard_rows, preferred_element_type=f32)
    grad_p = glu_back((new_block, grad_right))[0].astype(bf16)
    grad_proj = jnp.einsum("ijc,ijd->cd", in_normed, grad_p, preferred_element_type=f32) * inv_count
    grad_normed = jnp.dot(grad_p, in_proj.T, preferred_element_type=f32) + jnp.dot(
        grad_logit, in_gate.T, preferred_element_type=f32
    )
    grad_z, grad_norm = norm_back(grad_normed)
    pair_grad = (upstream + grad_z).astype(bf16)
    reduced = tuple(
        (
            part.astype(jnp.float32)
            for part in together(
                (
                    grad_proj.astype(jnp.bfloat16),
                    grad_gate.astype(jnp.bfloat16),
                    grad_final.astype(jnp.bfloat16),
                    (grad_norm * inv_count).astype(jnp.bfloat16),
                    (grad_mid * inv_count).astype(jnp.bfloat16),
                ),
                "dap",
            )
        )
    )
    return (pair_grad, reduced[0], reduced[1], reduced[2], reduced[3], reduced[4])


def solution(mesh):
    placed = (
        P("dap", "cplx", None),
        P("dap", "cplx", None),
        P("cplx"),
        P("cplx"),
        P(),
        P(),
        P(),
        P(),
        P(),
        P(),
        P(),
        P(),
        P(),
        P(),
        P(),
    )
    return jax.shard_map(
        shards,
        mesh=mesh,
        in_specs=placed,
        out_specs=(
            P("dap", "cplx", None),
            P("cplx", None),
            P("cplx", None),
            P("cplx", None),
            P("cplx"),
            P("cplx"),
        ),
        check_vma=False,
    )
```

profile of v0, /device:TPU:16, one launch (start us, length us, event | category | flops | bytes accessed | tf_op | source)
XLA Modules:
  0.0 930.9 jit_solution(3358620269729586650)
XLA Ops:
  7.3 0.8 dynamic_slice.7
  9.6 1.9 fusion.44
  11.6 2.3 multiply_reduce_fusion.4
  14.1 1.1 fusion.58
  15.2 1.5 fusion.31
  16.8 1.9 copy.47
  18.7 2.8 fusion.12
  21.5 204.7 %all-gather.4.cloned.1.call-done = bf16[192,192,128]{2,1,0:T(8,128)(2,1)} async-done(((bf16[12,192,128]{2,1,0:T(8,128)(2,1)}), bf16[192,192,128]{2,1,0:T(8,128)(2,1)}) %all-gather.4.cloned.1.call-update) | async-done | bytes 9437200 | tf_op jit(solution)/shard_map/all_gather | solution.py:74
  226.2 17.4 %copy.46 = bf16[192,192,128]{1,0,2:T(8,128)(2,1)} copy(bf16[192,192,128]{2,1,0:T(8,128)(2,1)} %all-gather.4.cloned.1.call-done) | data formatting | bytes 18874368 | tf_op jit(solution)/shard_map/all_gather | solution.py:74
  243.6 8.2 bitcast_reduce_fusion
  252.7 1.0 copy-done.8
  253.7 1.6 convert_reduce_fusion
  255.3 0.8 fusion.19
  256.1 0.8 fusion.62
  257.0 2.0 multiply_convert_fusion.2
  259.3 1.3 copy.49
  260.7 4.3 all-to-all-start
  266.0 41.9 %all-to-all-done = bf16[12,192,128]{2,0,1:T(8,128)(2,1)} async-done(((bf16[12,192,128]{2,0,1:T(8,128)(2,1)}), bf16[12,192,128]{2,0,1:T(8,128)(2,1)}, u32[]{:S(2)}, u32[]{:S(2)}) %all-to-all-start) | async-done | bytes 589856 | tf_op jit(solution)/shard_map/all_to_all | solution.py:91
  307.9 1.3 copy.51
  309.2 0.9 all_to_all.16
  310.2 1.8 copy.53
  312.0 163.0 %all-gather.6.cloned.1.call-done = bf16[192,192,128]{2,1,0:T(8,128)(2,1)} async-done(((bf16[12,192,128]{2,1,0:T(8,128)(2,1)}), bf16[192,192,128]{2,1,0:T(8,128)(2,1)}) %all-gather.6.cloned.1.call-update) | async-done | bytes 9437200 | tf_op jit(solution)/shard_map/all_gather | solution.py:96
  474.9 17.4 %copy.52 = bf16[192,192,128]{1,0,2:T(8,128)(2,1)} copy(bf16[192,192,128]{2,1,0:T(8,128)(2,1)} %all-gather.6.cloned.1.call-done) | data formatting | bytes 18874368 | tf_op jit(solution)/shard_map/all_gather | solution.py:96
  492.3 7.6 fusion.82
  500.0 2.2 copy.54
  503.3 1.3 multiply_reduce_fusion.3
  504.6 1.7 multiply_reduce_fusion.1
  506.3 2.3 add_convert_fusion.1
  509.0 2.6 copy.59
  511.6 2.6 copy.56
  514.2 2.7 fusion.15
  516.9 198.6 %all-gather.8.cloned.1.call-done = bf16[192,192,128]{2,1,0:T(8,128)(2,1)} async-done(((bf16[12,192,128]{2,1,0:T(8,128)(2,1)}), bf16[192,192,128]{2,1,0:T(8,128)(2,1)}) %all-gather.8.cloned.1.call-update) | async-done | bytes 9437200 | tf_op jit(solution)/shard_map/all_gather | solution.py:114
  715.5 17.4 %copy.55 = bf16[192,192,128]{1,0,2:T(8,128)(2,1)} copy(bf16[192,192,128]{2,1,0:T(8,128)(2,1)} %all-gather.8.cloned.1.call-done) | data formatting | bytes 18874368 | tf_op jit(solution)/shard_map/all_gather | solution.py:114
  732.9 9.5 %fusion.84 = f32[128,192,12]{1,2,0:T(8,128)} fusion(bf16[192,192,128]{1,0,2:T(8,128)(2,1)} %copy.55, bf16[12,192,128]{1,0,2:T(8,128)(2,1)} %copy.59), kind=kOutput, calls=%fused_computation.145 | convolution fusion | flops 113246208 | bytes 11206656 | tf_op jit(solution)/shard_map/kjc,ijc->kic/dot_general | solution.py:117
  742.4 2.7 copy.60
  745.1 7.9 fusion.83
  753.0 2.7 copy.57
  755.7 3.7 bitcast_multiply_fusion.3
  759.4 1.2 fusion.47
  761.7 1.0 fusion.52
  762.8 1.1 fusion.55
  763.8 0.8 fusion.20
  764.7 1.7 fusion.18
  767.6 2.5 fusion.22
  770.1 149.9 %all-reduce.6.cloned.1.call-done = bf16[98560]{0:T(1024)(128)(2,1)} async-done(((bf16[98560]{0:T(1024)(128)(2,1)}), bf16[98560]{0:T(1024)(128)(2,1)}) %all-reduce.6.cloned.1.call-update) | async-done | bytes 197136 | tf_op jit(solution)/shard_map/psum | solution.py:11
  920.0 0.9 slice_convert_fusion
  921.7 1.4 fusion.65
  923.1 1.3 slice_convert_fusion.1
  (74 shorter events, 8.4 us)
Async XLA Ops:
  7.2 249.0 %copy-start = (bf16[128,512]{1,0:T(8,128)(2,1)S(1)}, bf16[128,512]{1,0:T(8,128)(2,1)}, u32[]{:S(2)}) copy-start(bf16[128,512]{1,0:T(8,128)(2,1)} %param.26) | copy-start | bytes 393220
  7.2 6.9 copy-start.5
  7.2 6.7 copy-start.16
  7.2 6.8 copy-start.18
  7.2 6.8 copy-start.11
  7.2 218.9 %all-gather.4.cloned.1.call-start = ((), (), s32[]{:S(2)}) async-start(), calls=%async_computation.1 | async-start | bytes 10027008 | tf_op jit(solution)/shard_map/all_gather | solution.py:74
  16.7 2.0 copy-start.19
  16.7 458.2 %all-gather.6.cloned.1.call-start = ((), (), s32[]{:S(2)}) async-start(), calls=%async_computation.2 | async-start | bytes 10027008 | tf_op jit(solution)/shard_map/all_gather | solution.py:96
  251.7 0.7 copy-start.17
  252.4 1.3 copy-start.8
  252.4 1.3 copy-start.12
  253.7 2.5 copy-start.15
  257.0 2.3 copy-start.1
  259.3 1.3 copy-start.6
  259.3 5.8 copy-start.13
  260.7 47.2 %all-to-all-start = ((bf16[12,192,128]{2,0,1:T(8,128)(2,1)}), bf16[12,192,128]{2,0,1:T(8,128)(2,1)}, u32[]{:S(2)}, u32[]{:S(2)}) async-start(bf16[12,192,128]{2,0,1:T(8,128)(2,1)} %copy.49), calls=%async_computation | async-start | bytes 1572864 | tf_op jit(solution)/shard_map/all_to_all | solution.py:91
  264.9 450.6 %all-gather.8.cloned.1.call-start = ((), (), s32[]{:S(2)}) async-start(), calls=%async_computation.3 | async-start | bytes 10027008 | tf_op jit(solution)/shard_map/all_gather | solution.py:114
  502.2 1.1 copy-start.2
  502.2 1.1 copy-start.10
  502.3 1.0 copy-start.14
  508.7 411.3 %all-reduce.6.cloned.1.call-start = ((), (), s32[]{:S(2)}) async-start(), calls=%async_computation.4 | async-start | bytes 397312 | tf_op jit(solution)/shard_map/psum | solution.py:11
  760.7 1.1 copy-start.7
  761.5 1.2 copy-start.3
  764.7 2.9 copy-start.4
  766.9 0.7 copy-start.9
Sparse Core Ops, SparseCore 0:
  16.8 209.2 all-gather.3
  259.4 215.4 all-gather.5
  508.8 206.6 all-gather.7
  767.7 152.2 all-reduce.5
where the time goes:
time: 933 us; the launch traced here: 931 us
  waiting for transfers between devices  758 us (81%)
  local copies, waits for them, and re-layouts  78.5 us (8%)
  matrix products  49.2 us (5%)
  other arithmetic  26.1 us (3%)
  between operations  14.2 us (2%)
    all_gather x1, waiting for transfers between devices, shards(): lax.all_gather(right_b, 'dap', axis=0, tiled=True)  205 us
    all_gather x1, waiting for transfers between devices, shards(): shard_rows = lax.all_gather(grad_x_b, 'dap', axis=0, tiled=True)  199 us
    all_gather x1, waiting for transfers between devices, shards(): lax.all_gather(right_ib, 'dap', axis=0, tiled=True)  163 us
    psum x1, waiting for transfers between devices, together(): subtotal = lax.psum(jnp.concatenate([a.ravel() for a in arrays]), axis)  150 us
    all_to_all x1, waiting for transfers between devices, shards(): lax.all_to_all(left_ib, 'dap', split_axis=1, concat_axis=0, tiled=True)  41.9 us
  transfers between devices with their start and end apart: 5, of which 5 were waited for; matrix products, arithmetic and copies ran while one was open for 2% of the time, Pallas kernels for 0%

commit v1 on v0

v1 whole, which is shorter than its diff:
```python
import functools

import jax
import jax.numpy as jnp
from jax import lax
from jax.experimental import pallas as pl
from jax.experimental.pallas import tpu as pltpu
from jax.sharding import PartitionSpec as P

f32 = jnp.float32
bf16 = jnp.bfloat16

ROWS, RES, CH, DEV = 12, 192, 128, 16
CG = CH // DEV
STEPS = ROWS // 2
W = 2 * RES
PAIRS = ROWS * RES
HALF = PAIRS // 2
EPS = 1e-5
INV = 1.0 / RES
VM = pl.BlockSpec(memory_space=pltpu.VMEM)
LIMIT = 60 * 1024 * 1024


def dot(a, b, ca, cb):
    return lax.dot_general(a, b, (((ca,), (cb,)), ((), ())), preferred_element_type=f32)


def lanes_of(m, width=W):
    return pl.ds(pl.multiple_of(m * width, 128), width)


def norm_stats(v):
    mean = jnp.mean(v, axis=0, keepdims=True)
    cent = v - mean
    var = jnp.mean(cent * cent, axis=0, keepdims=True)
    rstd = lax.rsqrt(var + EPS)
    return cent * rstd, rstd


def sig(v):
    return jax.nn.sigmoid(v)


def to_channels(pair_ref, sel, m):
    two = pair_ref[pl.ds(2 * m, 2)].reshape(W, CH)
    return dot(two, sel, 0, 0)


def pre_kernel(pair_ref, sel_ref, rows_ref, vec_ref, w_ref, start_ref, gate_ref, ab_ref):
    def step(m, _):
        at = lanes_of(m)
        st = to_channels(pair_ref, sel_ref[...], m)
        same = rows_ref[1:2, at]
        st = st + jnp.where(same > 0.5, vec_ref[:, 1:2], vec_ref[:, 0:1])
        start_ref[:, at] = st
        xhat, _ = norm_stats(st)
        normed = (xhat * vec_ref[:, 2:3]).astype(bf16)
        p = dot(w_ref[...], normed, 1, 0)
        pm = rows_ref[0:1, at]
        ab = pm * sig(p[0:256]) * p[256:512]
        ab_ref[:, :, at] = ab.astype(bf16).reshape(DEV, 16, W)
        gate_ref[:, at] = sig(p[512:640])
        return 0

    lax.fori_loop(0, STEPS, step, 0)


def load_x(x_ref, m3):
    at = lanes_of(m3)
    both = x_ref[:, :, at].astype(f32)
    return [both[:, 8 * h : 8 * h + 8].reshape(CH, W) for h in (0, 1)]


def mid_kernel(x_ref, start_ref, gate_ref, rows_ref, vec_ref, wf_ref, w_ref, mid_ref, nrm_ref, ab_ref):
    def step(m3, _):
        for h, x in enumerate(load_x(x_ref, m3)):
            at = lanes_of(m3 + 3 * h)
            xhat, _ = norm_stats(x)
            y = (xhat * vec_ref[:, 3:4]).astype(bf16)
            upd = gate_ref[:, at] * dot(wf_ref[...], y, 1, 0)
            mid = (start_ref[:, at] + upd).astype(bf16)
            mid_ref[:, at] = mid
            zhat, _ = norm_stats(mid.astype(f32))
            normed = (zhat * vec_ref[:, 4:5]).astype(bf16)
            nrm_ref[:, at] = normed
            p = dot(w_ref[...], normed, 1, 0)
            ab = rows_ref[0:1, at] * sig(p[0:256]) * p[256:512]
            ab_ref[:, :, at] = ab.astype(bf16).reshape(DEV, 16, W)
        return 0

    lax.fori_loop(0, 3, step, 0)


def lane_sum(v):
    total = v[:, 0:128]
    for t in range(1, v.shape[1] // 128):
        total = total + v[:, 128 * t : 128 * t + 128]
    return total


def value_kernel(
    x_ref, ct_ref, nrm_ref, sel_ref, vec_ref, wgt_ref, wft_ref, wf_ref,
    gx_ref, gl_ref, ggate_ref, gfinal_ref, gmid_ref,
):
    ggate_ref[...] = jnp.zeros_like(ggate_ref)
    gfinal_ref[...] = jnp.zeros_like(gfinal_ref)
    gmid_ref[...] = jnp.zeros_like(gmid_ref)

    def step(m3, _):
        grads = []
        for h, x in enumerate(load_x(x_ref, m3)):
            m = m3 + 3 * h
            at = lanes_of(m)
            xhat, rstd = norm_stats(x)
            gain = vec_ref[:, 5:6]
            y = (xhat * gain).astype(bf16)
            normed = nrm_ref[:, at]
            ct = to_channels(ct_ref, sel_ref[...], m)
            s = sig(dot(wgt_ref[...], normed, 1, 0))
            value = dot(wft_ref[...], y, 1, 0)
            gv = (ct * s).astype(bf16)
            gl = (ct * value * s * (1.0 - s)).astype(bf16)
            gl_ref[:, at] = gl
            gfinal_ref[...] += dot(y, gv, 1, 1)
            ggate_ref[...] += dot(normed, gl, 1, 1)
            gy = dot(wf_ref[...], gv, 1, 0)
            gmid_ref[...] += lane_sum(gy * xhat)
            gh = gy * gain
            gx = rstd * (
                gh
                - jnp.mean(gh, axis=0, keepdims=True)
                - xhat * jnp.mean(gh * xhat, axis=0, keepdims=True)
            )
            grads.append(gx.reshape(DEV, CG, W))
        gx_ref[:, :, lanes_of(m3)] = jnp.concatenate(grads, axis=1).astype(bf16)
        return 0

    lax.fori_loop(0, 3, step, 0)


def post_kernel(
    gab_ref, ct_ref, mid_ref, nrm_ref, gl_ref, sel_ref, rows_ref, vec_ref, w_ref, wt_ref, wg_ref,
    out_ref, gproj_ref, gnorm_ref,
):
    gproj_ref[...] = jnp.zeros_like(gproj_ref)
    gnorm_ref[...] = jnp.zeros_like(gnorm_ref)

    def step(m, _):
        at = lanes_of(m)
        normed = nrm_ref[:, at]
        p = dot(w_ref[...], normed, 1, 0)
        g = sig(p[0:256])
        v = p[256:512]
        gab = gab_ref[:, :, at].reshape(256, W).astype(f32) * rows_ref[0:1, at]
        gp = jnp.concatenate([gab * v * g * (1.0 - g), gab * g], axis=0).astype(bf16)
        gproj_ref[...] += dot(gp, normed, 1, 1)
        gn = dot(wt_ref[...], gp, 1, 0) + dot(wg_ref[...], gl_ref[:, at], 1, 0)
        zhat, rstd = norm_stats(mid_ref[:, at].astype(f32))
        gnorm_ref[...] += lane_sum(gn * zhat)
        gh = gn * vec_ref[:, 4:5]
        gz = rstd * (
            gh
            - jnp.mean(gh, axis=0, keepdims=True)
            - zhat * jnp.mean(gh * zhat, axis=0, keepdims=True)
        )
        ct = to_channels(ct_ref, sel_ref[...], m)
        res = (ct + gz).astype(bf16)
        back = dot(sel_ref[...], res, 1, 1)
        out_ref[pl.ds(2 * m, 2)] = back.astype(bf16).reshape(2, RES, CH)
        return 0

    lax.fori_loop(0, STEPS, step, 0)


def peers():
    me = lax.axis_index("dap")
    mx, mz = me // 4, me % 4
    out = []
    for dz in (2, 3, 1, 0):
        for dx in range(4):
            if dx == 0 and dz == 0:
                continue
            out.append(
                (
                    ((mx + dx) % 4) * 4 + (mz + dz) % 4,
                    ((mx - dx) % 4) * 4 + (mz - dz) % 4,
                )
            )
    return me, out


def greet(out):
    barrier = pltpu.get_barrier_semaphore()
    for to, _ in out:
        pl.semaphore_signal(
            barrier, inc=1, device_id={"dap": to}, device_id_type=pl.DeviceIdType.MESH
        )
    pl.semaphore_wait(barrier, len(out))


def exchange(src_ref, dst_ref, me, out, send_sem, recv_sem):
    copies = []
    for i, (to, _) in enumerate(out):
        copy = pltpu.make_async_remote_copy(
            src_ref=src_ref.at[to],
            dst_ref=dst_ref.at[me],
            send_sem=send_sem.at[i],
            recv_sem=recv_sem.at[i],
            device_id={"dap": to},
            device_id_type=pl.DeviceIdType.MESH,
        )
        copy.start()
        copies.append(copy)
    return copies


def spread(src, wide_ref, s):
    rows = pl.ds(pl.multiple_of(s * 16, 16), 16)
    for t in range(wide_ref.shape[0]):
        wide_ref[t, rows, :] = src[:, 128 * t : 128 * t + 128].astype(f32)


def low_lanes():
    return lax.broadcasted_iota(jnp.int32, (16, 128), 1) < 64


def gather_rows(wide_ref, first, m, stride, mat_ref, c, col):
    low = low_lanes()
    rows = pl.ds(first, 16, stride=stride)
    t0 = wide_ref[col, rows, :]
    t1 = wide_ref[col + 1, rows, :]
    t2 = wide_ref[col + 2, rows, :]
    r = 32 * m
    mat_ref[c, r : r + 16, 0:128] = t0.astype(bf16)
    mat_ref[c, r + 16 : r + 32, 0:128] = t1.astype(bf16)
    mat_ref[c, r : r + 16, 128:256] = jnp.where(low, t2, 0.0).astype(bf16)
    mat_ref[c, r + 16 : r + 32, 128:256] = jnp.where(low, pltpu.roll(t2, 64, 1), 0.0).astype(bf16)


def scatter_rows(res, m, wide_ref, first, stride, col):
    low = low_lanes()
    rows = pl.ds(first, 16, stride=stride)
    r = 32 * m
    wide_ref[col, rows, :] = res[r : r + 16, 0:128]
    wide_ref[col + 1, rows, :] = res[r + 16 : r + 32, 0:128]
    odd = pltpu.roll(res[r + 16 : r + 32, 128:256], 64, 1)
    wide_ref[col + 2, rows, :] = jnp.where(low, res[r : r + 16, 128:256], odd)


def clear_tail(ref):
    ref[:, RES:256, :] = jnp.zeros((CG, 256 - RES, 256), bf16)


def tri_kernel(transposed, ab_ref, x_ref, a_ref, b_ref, recv, wide, xwide, xs, s1, r1, s2, r2):
    me, out = peers()
    greet(out)
    copies = exchange(ab_ref, recv, me, out, s1, r1)
    clear_tail(a_ref)
    clear_tail(b_ref)
    spread(ab_ref[me], wide, me)
    for copy, (_, frm) in zip(copies, out):
        copy.wait_recv()
        spread(recv[frm], wide, frm)

    def channel(c, _):
        for m in range(STEPS):
            gather_rows(wide, c, m, 16, a_ref, c, 3 * m)
            gather_rows(wide, CG + c, m, 16, b_ref, c, 3 * m)
        k = 0 if transposed else 1
        res = dot(a_ref[c], b_ref[c], k, k)
        for m in range(STEPS):
            scatter_rows(res, m, xwide, c + CG * (m // 3), 16, 3 * (m % 3))
        return 0

    lax.fori_loop(0, CG, channel, 0)
    for copy in copies:
        copy.wait_send()
    for s in range(DEV):
        for t in range(9):
            xs[s, :, 128 * t : 128 * t + 128] = xwide[t, 16 * s : 16 * s + 16, :].astype(bf16)
    back = exchange(xs, x_ref, me, out, s2, r2)
    x_ref[me] = xs[me]
    for copy in back:
        copy.wait()


def grad_kernel(gx_ref, a_ref, b_ref, gab_ref, recv, wide, gmat, gwide, gs, s1, r1, s2, r2):
    me, out = peers()
    greet(out)
    copies = exchange(gx_ref, recv, me, out, s1, r1)
    clear_tail(gmat)
    spread(gx_ref[me], wide, me)
    for copy, (_, frm) in zip(copies, out):
        copy.wait_recv()
        spread(recv[frm], wide, frm)

    def channel(c, _):
        for m in range(STEPS):
            gather_rows(wide, c + CG * (m // 3), m, 16, gmat, c, 3 * (m % 3))
        ga = dot(b_ref[c], gmat[c], 1, 1)
        gb = dot(a_ref[c], gmat[c], 1, 0)
        for m in range(STEPS):
            scatter_rows(ga, m, gwide, c, 16, 3 * m)
            scatter_rows(gb, m, gwide, CG + c, 16, 3 * m)
        return 0

    lax.fori_loop(0, CG, channel, 0)
    for copy in copies:
        copy.wait_send()
    for s in range(DEV):
        for t in range(18):
            gs[s, :, 128 * t : 128 * t + 128] = gwide[t, 16 * s : 16 * s + 16, :].astype(bf16)
    back = exchange(gs, gab_ref, me, out, s2, r2)
    gab_ref[me] = gs[me]
    for copy in back:
        copy.wait()


def sum_kernel(part_ref, full_ref, vec_ref, recv, red, s1, r1, s2, r2):
    me, out = peers()
    greet(out)
    copies = exchange(part_ref, recv, me, out, s1, r1)
    recv[me] = part_ref[me]
    for copy in copies:
        copy.wait()
    total = recv[0].astype(f32)
    for s in range(1, DEV):
        total = total + recv[s].astype(f32)
    vec_ref[...] = total[48:64]
    red[...] = total[0:48].astype(bf16)
    back = []
    for i, (to, _) in enumerate(out):
        copy = pltpu.make_async_remote_copy(
            src_ref=red,
            dst_ref=full_ref.at[me],
            send_sem=s2.at[i],
            recv_sem=r2.at[i],
            device_id={"dap": to},
            device_id_type=pl.DeviceIdType.MESH,
        )
        copy.start()
        back.append(copy)
    full_ref[me] = red[...]
    for copy in back:
        copy.wait()


def shape(dims, dtype):
    return jax.ShapeDtypeStruct(dims, dtype)


def local_call(kernel, outs, *args):
    return pl.pallas_call(
        kernel,
        out_shape=outs,
        in_specs=[VM] * len(args),
        out_specs=[VM] * len(outs),
        compiler_params=pltpu.CompilerParams(vmem_limit_bytes=LIMIT),
    )(*args)


def link_call(kernel, outs, scratch, ident, *args):
    sems = [pltpu.SemaphoreType.DMA((DEV - 1,))] * 4
    return pl.pallas_call(
        kernel,
        out_shape=outs,
        in_specs=[VM] * len(args),
        out_specs=[VM] * len(outs),
        scratch_shapes=list(scratch) + sems,
        compiler_params=pltpu.CompilerParams(
            vmem_limit_bytes=LIMIT, collective_id=ident, has_side_effects=True
        ),
    )(*args)


def split_order(proj):
    return proj.reshape(CH, 2, 2, DEV, CG).transpose(2, 3, 1, 4, 0).reshape(4 * CH, CH)


def lane_order(rows, cols):
    order = cols.reshape(DEV, ROWS).T.reshape(RES)
    r = rows.reshape(STEPS, 2)
    row = jnp.concatenate(
        [jnp.broadcast_to(r[:, 0:1], (STEPS, 128)), jnp.broadcast_to(r[:, 1:2], (STEPS, 128)),
         jnp.broadcast_to(r[:, 0:1], (STEPS, 64)), jnp.broadcast_to(r[:, 1:2], (STEPS, 64))], axis=1)
    col = jnp.concatenate([order[:128], order[:128], order[128:], order[128:]])
    return row, jnp.broadcast_to(col[None], (STEPS, W))


def selector():
    lane = lax.broadcasted_iota(jnp.int32, (W, W), 1)
    src = lax.broadcasted_iota(jnp.int32, (W, W), 0)
    tail = lane - 256
    i = jnp.where(lane < 256, lane // 128, tail // 64)
    pos = jnp.where(lane < 256, lane % 128, 128 + tail % 64)
    res = (pos % DEV) * ROWS + pos // DEV
    return (src == i * RES + res).astype(bf16)


def shards(
    pair, cotangent, residue_mask, chain_ids, chain_embed, out_norm_gain, out_proj, out_gate,
    out_mid_gain, out_final, in_norm_gain, in_proj, in_gate, in_mid_gain, in_final,
):
    first = lax.axis_index("dap") * ROWS
    row_mask = lax.dynamic_slice_in_dim(residue_mask, first, ROWS, 0)
    row_chain = lax.dynamic_slice_in_dim(chain_ids, first, ROWS, 0)
    mr, mc = lane_order(row_mask, residue_mask)
    cr, cc = lane_order(row_chain, chain_ids)
    rows = jnp.stack([(mr * mc).astype(f32).reshape(PAIRS), (cr == cc).astype(f32).reshape(PAIRS)])
    zero = jnp.zeros_like(out_norm_gain)
    vec = jnp.stack(
        [chain_embed[0], chain_embed[1], out_norm_gain, out_mid_gain, in_norm_gain, in_mid_gain, zero, zero],
        axis=1,
    )
    sel = selector()
    w_out = jnp.concatenate([split_order(out_proj), out_gate.T], axis=0)
    w_in = split_order(in_proj)

    start, gate, ab = local_call(
        pre_kernel,
        [shape((CH, PAIRS), f32), shape((CH, PAIRS), f32), shape((DEV, 16, PAIRS), bf16)],
        pair, sel, rows, vec, w_out,
    )
    tri_scratch = [
        pltpu.VMEM((DEV, 16, PAIRS), bf16),
        pltpu.VMEM((18, DEV * 16, 128), f32),
        pltpu.VMEM((9, DEV * 16, 128), f32),
        pltpu.VMEM((DEV, 16, HALF), bf16),
    ]
    tri_out = [shape((DEV, 16, HALF), bf16), shape((CG, 256, 256), bf16), shape((CG, 256, 256), bf16)]
    x, _, _ = link_call(functools.partial(tri_kernel, False), tri_out, tri_scratch, 0, ab)
    mid, nrm, ab = local_call(
        mid_kernel,
        [shape((CH, PAIRS), bf16), shape((CH, PAIRS), bf16), shape((DEV, 16, PAIRS), bf16)],
        x, start, gate, rows, vec, out_final.T, w_in,
    )
    x, a, b = link_call(functools.partial(tri_kernel, True), tri_out, tri_scratch, 1, ab)
    gx, gl, ggate, gfinal, gmid = local_call(
        value_kernel,
        [shape((DEV, 16, HALF), bf16), shape((CH, PAIRS), bf16), shape((CH, CH), f32),
         shape((CH, CH), f32), shape((CH, 128), f32)],
        x, cotangent, nrm, sel, vec, in_gate.T, in_final.T, in_final,
    )
    (gab,) = link_call(
        grad_kernel,
        [shape((DEV, 16, PAIRS), bf16)],
        [
            pltpu.VMEM((DEV, 16, HALF), bf16),
            pltpu.VMEM((9, DEV * 16, 128), f32),
            pltpu.VMEM((CG, 256, 256), bf16),
            pltpu.VMEM((18, DEV * 16, 128), f32),
            pltpu.VMEM((DEV, 16, PAIRS), bf16),
        ],
        2, gx, a, b,
    )
    pair_grad, gproj, gnorm = local_call(
        post_kernel,
        [shape((ROWS, RES, CH), bf16), shape((4 * CH, CH), f32), shape((CH, 128), f32)],
        gab, cotangent, mid, nrm, gl, sel, rows, vec, w_in, w_in.T, in_gate,
    )

    flat = jnp.concatenate([gproj, ggate, gfinal], axis=0) * INV
    gains = jnp.stack([jnp.sum(gnorm, axis=1), jnp.sum(gmid, axis=1)]) * INV
    gains = jnp.concatenate([gains, jnp.zeros((14, CH), f32)], axis=0)
    part = jnp.concatenate(
        [flat.reshape(DEV, 48, CH), jnp.broadcast_to(gains[None], (DEV, 16, CH))], axis=1
    ).astype(bf16)
    full, gvec = link_call(
        sum_kernel,
        [shape((DEV, 48, CH), bf16), shape((16, CH), f32)],
        [pltpu.VMEM((DEV, 64, CH), bf16), pltpu.VMEM((48, CH), bf16)],
        3, part,
    )
    full = full.reshape(6 * CH, CH).astype(f32)
    grad_proj = (
        full[: 4 * CH].reshape(2, DEV, 2, CG, CH).transpose(4, 2, 0, 1, 3).reshape(CH, 4 * CH)
    )
    return (pair_grad, grad_proj, full[4 * CH : 5 * CH], full[5 * CH :], gvec[0], gvec[1])


def solution(mesh):
    whole = P()
    placed = (P("dap", "cplx", None), P("dap", "cplx", None), P("cplx"), P("cplx")) + (whole,) * 11
    return jax.shard_map(
        shards,
        mesh=mesh,
        in_specs=placed,
        out_specs=(
            P("dap", "cplx", None),
            P("cplx", None),
            P("cplx", None),
            P("cplx", None),
            P("cplx"),
            P("cplx"),
        ),
        check_vma=False,
    )
```

time: 933 us -> 214 us (0.23)
  waiting for transfers between devices: 758 us -> 0 us
  Pallas kernels: 0 us -> 188 us
  local copies, waits for them, and re-layouts: 78.5 us -> 14.8 us
  matrix products: 49.2 us -> 0 us
  other arithmetic: 26.1 us -> 6.23 us
  between operations: 14.2 us -> 0.89 us
    all_gather x3 -> x0, waiting for transfers between devices: 566 us -> none  [the longest x1 205 us: shards(): lax.all_gather(right_b, 'dap', axis=0, tiled=True)]
    pallas_call x0 -> x8, Pallas kernels: none -> 188 us  [the longest x4 162 us: link_call(): pl.pallas_call(kernel, out_shape=outs, in_specs=[VM] * len(args), out_spe...]
    psum x1 -> x0, waiting for transfers between devices: 150 us -> none  [together(): subtotal = lax.psum(jnp.concatenate([a.ravel() for a in arrays]), axis)]
    all_gather x3 -> x0, local copies, waits for them, and re-layouts: 52.2 us -> none  [the longest x1 17.4 us: shards(): shard_rows = lax.all_gather(grad_x_b, 'dap', axis=0, tiled=True)]
    dot_general x16 -> x0, matrix products: 49.2 us -> none  [the longest x1 9.51 us: shards(): jnp.einsum('kjc,ijc->kic', right_ib, shard_rows, preferred_element_type=f32)]
    all_to_all x1 -> x0, waiting for transfers between devices: 41.9 us -> none  [shards(): lax.all_to_all(left_ib, 'dap', split_axis=1, concat_axis=0, tiled=True)]
    convert_element_type x11 -> x2, other arithmetic: 12.2 us -> 1.77 us  [the longest x1 0.95 us: shards(): full = full.reshape(6 * CH, CH).astype(f32)]
  transfers between devices with their start and end apart: 5 -> 0, of which waited for: 5 -> 0; matrix products, arithmetic and copies ran while one was open for 2% -> 0% of each run, Pallas kernels for 0% -> 0%
where the time goes in v1:
time: 214 us; the launch traced here: 210 us
  Pallas kernels  188 us (88%)
  local copies, waits for them, and re-layouts  14.8 us (7%)
  other arithmetic  6.23 us (3%)
    pallas_call x4, Pallas kernels, link_call(): pl.pallas_call(kernel, out_shape=outs, in_specs=[VM] * len(args), out_spe...  162 us
    pallas_call x4, Pallas kernels, local_call(): pl.pallas_call(kernel, out_shape=outs, in_specs=[VM] * len(args), out_spe...  25.4 us
    unnamed x27, local copies, waits for them, and re-layouts  4.31 us

profile of v1, /device:TPU:16, one launch (start us, length us, event | category | flops | bytes accessed | tf_op | source)
XLA Modules:
  0.0 209.8 jit_solution(2913227854500422750)
XLA Ops:
  0.6 0.8 dynamic_slice.6
  1.4 0.1 reshape.108
  1.5 0.2 slice_reduce_fusion.3
  1.9 0.8 reshape.109
  2.8 0.1 copy.78
  2.9 0.1 slice.70
  3.0 0.1 slice.68
  3.1 0.1 pad_add_fusion
  3.2 0.1 fusion.12
  3.3 0.8 dynamic_slice.7
  4.1 0.1 reshape.110
  4.1 0.2 slice_reduce_fusion.1
  4.6 0.8 reshape.111
  5.4 0.1 copy.80
  5.5 0.1 slice.76
  5.7 0.1 slice.74
  5.8 0.1 pad_add_fusion.1
  5.8 0.1 convert_bitcast_fusion
  5.9 0.6 pad_maximum_fusion.2.rows_ref
  6.6 0.8 fusion.9.sel_ref
  7.5 0.8 slice_bitcast_fusion.2
  8.2 0.7 stack.36
  8.9 0.7 copy.84.vec_ref
  9.7 1.0 copy.81
  10.7 0.1 copy.83
  10.9 0.7 pad_maximum_fusion.1.w_ref
  11.5 6.3 %shard_map.190 = (f32[128,2304]{1,0:T(8,128)}, f32[128,2304]{1,0:T(8,128)}, bf16[16,16,2304]{2,1,0:T(8,128)(2,1)}) custom-call(bf16[12,192,128]{2,1,0:T(8,128)(2,1)} %pair_ref.1, bf16[384,384]{1,0:T(8,128)(2,1)} %fusion.9.sel_ref, f32[2,2304]{1,0:T(2,128)} %pad_maximum_fusion.2.rows_ref, f32[128,8]{1,0:T(8,128)} %copy.84.vec_ref, ...), custom_call_target="tpu_custom_call" | custom-call | tf_op jit(solution)/shard_map/pallas_call | solution.py:354
  17.8 52.6 %shard_map.191 = (bf16[16,16,1152]{2,1,0:T(8,128)(2,1)}, bf16[8,256,256]{2,1,0:T(8,128)(2,1)}, bf16[8,256,256]{2,1,0:T(8,128)(2,1)}) custom-call(bf16[16,16,2304]{2,1,0:T(8,128)(2,1)} %get-tuple-element.26.ab_ref), custom_call_target="tpu_custom_call" | custom-call | tf_op jit(solution)/shard_map/pallas_call | solution.py:365
  70.4 0.1 copy.86
  70.6 0.7 copy.87
  71.2 0.7 copy.85
  72.0 5.7 %shard_map.192 = (bf16[128,2304]{1,0:T(8,128)(2,1)}, bf16[128,2304]{1,0:T(8,128)(2,1)}, bf16[16,16,2304]{2,1,0:T(8,128)(2,1)}) custom-call(bf16[16,16,1152]{2,1,0:T(8,128)(2,1)} %get-tuple-element.27.x_ref, f32[128,2304]{1,0:T(8,128)} %get-tuple-element.28.start_ref, f32[128,2304]{1,0:T(8,128)} %get-tuple-element.29.gate_ref, ...), custom_call_target="tpu_custom_call" | custom-call | tf_op jit(solution)/shard_map/pallas_call | solution.py:354
  77.7 47.1 %shard_map.193 = (bf16[16,16,1152]{2,1,0:T(8,128)(2,1)}, bf16[8,256,256]{2,1,0:T(8,128)(2,1)}, bf16[8,256,256]{2,1,0:T(8,128)(2,1)}) custom-call(bf16[16,16,2304]{2,1,0:T(8,128)(2,1)} %get-tuple-element.30.ab_ref), custom_call_target="tpu_custom_call" | custom-call | tf_op jit(solution)/shard_map/pallas_call | solution.py:365
  124.8 0.7 copy.89
  125.6 0.7 copy.90
  126.3 5.2 %shard_map.194 = (bf16[16,16,1152]{2,1,0:T(8,128)(2,1)}, bf16[128,2304]{1,0:T(8,128)(2,1)}, f32[128,128]{1,0:T(8,128)}, f32[128,128]{1,0:T(8,128)}, f32[128,128]{1,0:T(8,128)}) custom-call(bf16[16,16,1152]{2,1,0:T(8,128)(2,1)} %get-tuple-element.31.x_ref, bf16[12,192,128]{2,1,0:T(8,128)(2,1)} %ct_ref.3, bf16[128,2304]{1,0:T(8,128)(2,1)} %get-tuple-element.32.nrm_ref, ...), custom_call_target="tpu_custom_call" | custom-call | tf_op jit(solution)/shard_map/pallas_call | solution.py:354
  131.5 40.7 %shard_map.195.gab_ref = bf16[16,16,2304]{2,1,0:T(8,128)(2,1)} custom-call(bf16[16,16,1152]{2,1,0:T(8,128)(2,1)} %get-tuple-element.33.gx_ref, bf16[8,256,256]{2,1,0:T(8,128)(2,1)} %get-tuple-element.34.a_ref, bf16[8,256,256]{2,1,0:T(8,128)(2,1)} %get-tuple-element.35.b_ref), custom_call_target="tpu_custom_call" | custom-call | tf_op jit(solution)/shard_map/pallas_call | solution.py:365
  172.2 0.8 copy.92
  173.0 8.2 %shard_map.196 = (bf16[12,192,128]{2,1,0:T(8,128)(2,1)}, f32[512,128]{1,0:T(8,128)}, f32[128,128]{1,0:T(8,128)}) custom-call(bf16[16,16,2304]{2,1,0:T(8,128)(2,1)} %shard_map.195.gab_ref, bf16[12,192,128]{2,1,0:T(8,128)(2,1)} %ct_ref.3, bf16[128,2304]{1,0:T(8,128)(2,1)} %get-tuple-element.36.mid_ref, bf16[128,2304]{1,0:T(8,128)(2,1)} %get-tuple-element.32.nrm_ref, ...), custom_call_target="tpu_custom_call" | custom-call | tf_op jit(solution)/shard_map/pallas_call | solution.py:354
  181.2 1.0 fusion.10
  182.2 0.9 reduce_sum.18
  183.2 0.1 reduce_sum.19
  183.3 0.7 pad_maximum_fusion.part_ref
  184.0 22.0 %shard_map.197 = (bf16[16,48,128]{2,1,0:T(8,128)(2,1)}, f32[16,128]{1,0:T(8,128)}) custom-call(bf16[16,64,128]{2,1,0:T(8,128)(2,1)} %pad_maximum_fusion.part_ref), custom_call_target="tpu_custom_call" | custom-call | tf_op jit(solution)/shard_map/pallas_call | solution.py:365
  206.1 1.0 bitcast_convert_fusion
  207.1 0.8 copy.95
  207.9 0.7 fusion.25
  208.6 1.3 slice_bitcast_fusion
  (46 shorter events, 1.1 us)
Async XLA Ops:
  0.6 10.1 %copy-start.7 = (bf16[128,128]{1,0:T(8,128)(2,1)S(1)}, bf16[128,128]{1,0:T(8,128)(2,1)}, u32[]{:S(2)}) copy-start(bf16[128,128]{1,0:T(8,128)(2,1)} %param.22) | copy-start | bytes 98308
  11.5 58.9 %copy-start.3 = (bf16[128,512]{1,0:T(8,128)(2,1)S(1)}, bf16[128,512]{1,0:T(8,128)(2,1)}, u32[]{:S(2)}) copy-start(bf16[128,512]{1,0:T(8,128)(2,1)} %param.26) | copy-start | bytes 393220
  11.5 59.7 %copy-start.8 = (bf16[128,128]{1,0:T(8,128)(2,1)S(1)}, bf16[128,128]{1,0:T(8,128)(2,1)}, u32[]{:S(2)}) copy-start(bf16[128,128]{1,0:T(8,128)(2,1)} %param.24) | copy-start | bytes 98308
  77.7 47.1 %copy-start.2 = (bf16[128,128]{1,0:T(8,128)(2,1)S(1)}, bf16[128,128]{1,0:T(8,128)(2,1)}, u32[]{:S(2)}) copy-start(bf16[128,128]{1,0:T(8,128)(2,1)} %wg_ref.1) | copy-start | bytes 98308
  77.7 47.9 %copy-start.1 = (bf16[128,128]{1,0:T(8,128)(2,1)S(1)}, bf16[128,128]{1,0:T(8,128)(2,1)}, u32[]{:S(2)}) copy-start(bf16[128,128]{1,0:T(8,128)(2,1)} %wf_ref.1) | copy-start | bytes 98308
  131.5 40.7 %copy-start = (bf16[2,16,2,8,128]{4,3,2,1,0:T(8,128)(2,1)S(1)}, bf16[2,16,2,8,128]{4,3,2,1,0:T(8,128)(2,1)}, u32[]{:S(2)}) copy-start(bf16[2,16,2,8,128]{4,3,2,1,0:T(8,128)(2,1)} %copy.87) | copy-start | bytes 393220
  173.0 8.2 %copy-start.4 = (f32[128,128]{1,0:T(8,128)S(1)}, f32[128,128]{1,0:T(8,128)}, u32[]{:S(2)}) copy-start(f32[128,128]{1,0:T(8,128)} %get-tuple-element.40) | copy-start | bytes 196612
  173.0 8.2 %copy-start.5 = (f32[128,128]{1,0:T(8,128)S(1)}, f32[128,128]{1,0:T(8,128)}, u32[]{:S(2)}) copy-start(f32[128,128]{1,0:T(8,128)} %get-tuple-element.41) | copy-start | bytes 196612
  173.0 10.2 %copy-start.6 = (f32[128,128]{1,0:T(8,128)S(1)}, f32[128,128]{1,0:T(8,128)}, u32[]{:S(2)}) copy-start(f32[128,128]{1,0:T(8,128)} %get-tuple-element.43) | copy-start | bytes 196612

commit v2 on v0

v2 whole, which is shorter than its diff:
```python
import jax
import jax.numpy as jnp
from jax import lax
from jax.experimental import pallas as pl
from jax.experimental.pallas import tpu as pltpu
from jax.sharding import PartitionSpec as P

f32 = jnp.float32
bf16 = jnp.bfloat16

ROWS, RES, CH, DEV = 12, 192, 128, 16
CG = CH // DEV
W = 2 * RES
CHUNKS = 3
LANES = 2 * W
EPS = 1e-5
INV = 1.0 / RES
MESH = pl.DeviceIdType.MESH


def dot(a, b, ca, cb):
    return lax.dot_general(a, b, (((ca,), (cb,)), ((), ())), preferred_element_type=f32)


def norm_stats(v):
    mean = jnp.mean(v, axis=0, keepdims=True)
    cent = v - mean
    var = jnp.mean(cent * cent, axis=0, keepdims=True)
    rstd = lax.rsqrt(var + EPS)
    return cent * rstd, rstd


def norm_grad(gh, xhat, rstd):
    return rstd * (
        gh
        - jnp.mean(gh, axis=0, keepdims=True)
        - xhat * jnp.mean(gh * xhat, axis=0, keepdims=True)
    )


def sig(v):
    return jax.nn.sigmoid(v)


def lane_sum(v):
    total = v[:, 0:128]
    for t in range(1, v.shape[1] // 128):
        total = total + v[:, 128 * t : 128 * t + 128]
    return total


def low(rows):
    return lax.broadcasted_iota(jnp.int32, (rows, 128), 1) < 64


def swap(v):
    return pltpu.roll(v, 64, 1)


def selector():
    lane = lax.broadcasted_iota(jnp.int32, (W, W), 1)
    src = lax.broadcasted_iota(jnp.int32, (W, W), 0)
    tail = lane - 256
    first = lane < 256
    i = jnp.where(first, lane >> 7, tail >> 6)
    pos = jnp.where(first, lane & 127, 128 + (tail & 63))
    res = (pos & (DEV - 1)) * ROWS + (pos >> 4)
    return jnp.where(src == i * RES + res, 1.0, 0.0).astype(bf16)


def turn(w):
    return w.astype(f32).T.astype(bf16)


def kernel(
    pair, cot, mask_row, chain_row, mask_s, chain_s, embed, gain0, gain1, gain2, gain3,
    w_out, w_og, w_of, w_in, w_ig, w_if,
    out, o_proj, o_gate, o_final, o_norm, o_mid,
    sel, vecs, cols, wt_out, wt_og, wt_of, wt_in, wt_ig, wt_if,
    start, gate, mid, nrm, gl, cott,
    b1s, a1s, x1s, b2s, a2s, x2s, gxs, gas, gbs, p1s, p2s, g1s, g2s,
    b1r, a1r, x1r, b2r, a2r, x2r, gxr, gar, gbr, p1r, p2r, g1r, g2r,
    wide, back, am, bm, aq, b2, gq, acc_proj, acc_gate, acc_final, acc_norm, acc_mid,
    send_sem, recv_sem,
):
    me = lax.axis_index("dap")
    mx, mz = me // 4, me % 4

    def peer(i):
        o = 15 - i
        return ((mx + o % 4) % 4) * 4 + (mz + o // 4) % 4

    barrier = pltpu.get_barrier_semaphore()

    def greet(i, _):
        pl.semaphore_signal(barrier, inc=1, device_id={"dap": peer(i)}, device_id_type=MESH)
        return 0

    lax.fori_loop(0, DEV - 1, greet, 0)

    def send(src, dst, r, ident):
        def one(i, _):
            to = peer(i)
            pltpu.make_async_remote_copy(
                src_ref=src.at[r, to],
                dst_ref=dst.at[r, me],
                send_sem=send_sem.at[ident, r],
                recv_sem=recv_sem.at[ident, r],
                device_id={"dap": to},
                device_id_type=MESH,
            ).start()
            return 0

        lax.fori_loop(0, DEV - 1, one, 0)
        dst[r, me] = src[r, me]

    def share(src, dst, ident):
        def one(i, _):
            pltpu.make_async_remote_copy(
                src_ref=src,
                dst_ref=dst.at[me],
                send_sem=send_sem.at[ident, 0],
                recv_sem=recv_sem.at[ident, 0],
                device_id={"dap": peer(i)},
                device_id_type=MESH,
            ).start()
            return 0

        lax.fori_loop(0, DEV - 1, one, 0)
        dst[me] = src[...]

    def wait(dst, r, ident):
        blocks = dst.at[r, pl.ds(0, DEV - 1)]
        pltpu.make_async_copy(blocks, blocks, recv_sem.at[ident, r]).wait()

    sel[...] = selector()
    vecs[...] = jnp.zeros_like(vecs)
    vecs[0:2, :] = embed[...]
    vecs[2:3, :] = gain0[...]
    vecs[3:4, :] = gain1[...]
    vecs[4:5, :] = gain2[...]
    vecs[5:6, :] = gain3[...]
    cols[...] = vecs[...].T
    for t in range(4):
        wt_out[128 * t : 128 * t + 128, :] = turn(w_out[:, 128 * t : 128 * t + 128])
    wt_og[...] = turn(w_og[...])

    def by_lane(row_ref):
        wide_row = jnp.broadcast_to(row_ref[...].astype(f32), (16, RES)).astype(bf16)
        return (dot(wide_row, sel[0:RES, :], 1, 0) + dot(wide_row, sel[RES:W, :], 1, 0))[0:1]

    lane = lax.broadcasted_iota(jnp.int32, (1, W), 1)
    second = jnp.where(lane < 256, lane >> 7, (lane - 256) >> 6) == 1
    lane_mask = by_lane(mask_row)
    lane_chain = by_lane(chain_row)

    def row_pair(ref, m):
        at = me * ROWS + 2 * m
        return jnp.where(second, ref[0, at + 1].astype(f32), ref[0, at].astype(f32))

    def pair_mask(m):
        return row_pair(mask_s, m) * lane_mask

    def to_channels(ref, m):
        return dot(ref[pl.ds(2 * m, 2)].reshape(W, CH), sel[...], 0, 0)

    def blocks(v):
        return v.reshape(DEV, CG, v.shape[1]).astype(bf16)

    pl.semaphore_wait(barrier, DEV - 1)

    def project(r, _):
        for mm in (0, 1):
            m = 2 * r + mm
            at = slice(W * mm, W * mm + W)
            same = row_pair(chain_s, m) == lane_chain
            st = to_channels(pair, m) + jnp.where(same, cols[:, 1:2], cols[:, 0:1])
            start[m] = st
            xhat, _ = norm_stats(st)
            normed = (xhat * cols[:, 2:3]).astype(bf16)
            p = dot(wt_out[...], normed, 1, 0)
            pm = pair_mask(m)
            b1s[r, :, :, at] = blocks(pm * sig(p[256:384]) * p[384:512])
            a1s[r, :, :, at] = blocks(pm * sig(p[0:128]) * p[128:256])
            gate[m] = sig(dot(wt_og[...], normed, 1, 0))
        send(b1s, b1r, r, 0)
        return 0

    lax.fori_loop(0, CHUNKS, project, 0)

    def send_all(src, dst, ident):
        def one(r, _):
            send(src, dst, r, ident)
            return 0

        lax.fori_loop(0, CHUNKS, one, 0)

    send_all(a1s, a1r, 1)

    for t in range(4):
        wt_in[128 * t : 128 * t + 128, :] = turn(w_in[:, 128 * t : 128 * t + 128])
    wt_of[...] = turn(w_of[...])
    wt_ig[...] = turn(w_ig[...])
    wt_if[...] = turn(w_if[...])

    def turn_cot(m, _):
        cott[m] = to_channels(cot, m).astype(bf16)
        return 0

    lax.fori_loop(0, 2 * CHUNKS, turn_cot, 0)
    bm[:, RES:256, :] = jnp.zeros((CG, 256 - RES, 256), bf16)
    gq[...] = jnp.zeros_like(gq)

    def widen(src, r):
        for t in range(LANES // 128):
            wide[t] = src[r, :, :, 128 * t : 128 * t + 128].astype(f32).reshape(CH, 128)

    def fill_rows(c, put):
        pick = pl.ds(c, DEV, stride=CG)
        lo = low(DEV)
        for mm in (0, 1):
            tail = wide[3 * mm + 2, pick, :]
            put(32 * mm, wide[3 * mm, pick, :], jnp.where(lo, tail, 0.0))
            put(32 * mm + 16, wide[3 * mm + 1, pick, :], jnp.where(lo, swap(tail), 0.0))

    def rows_into(mat, r, c):
        base = r * 64

        def put(row, head, tail):
            at = pl.ds(pl.multiple_of(base + row, 16), 16)
            mat[c, at, 0:128] = head.astype(bf16)
            mat[c, at, 128:256] = tail.astype(bf16)

        fill_rows(c, put)

    def take_rows(src, r, mat):
        widen(src, r)

        def one(c, _):
            rows_into(mat, r, c)
            return 0

        lax.fori_loop(0, CG, one, 0)

    def rows_out(res, c):
        pick = pl.ds(c, DEV, stride=CG)
        lo = low(DEV)
        for mm in (0, 1):
            r = 32 * mm
            back[3 * mm, pick, :] = res[r : r + 16, 0:128]
            back[3 * mm + 1, pick, :] = res[r + 16 : r + 32, 0:128]
            back[3 * mm + 2, pick, :] = jnp.where(
                lo, res[r : r + 16, 128:256], swap(res[r + 16 : r + 32, 128:256])
            )

    def flush(dst, r):
        for t in range(LANES // 128):
            dst[r, :, :, 128 * t : 128 * t + 128] = back[t].reshape(DEV, CG, 128).astype(bf16)

    def take_b1(r, _):
        wait(b1r, r, 0)
        take_rows(b1r, r, bm)
        return 0

    lax.fori_loop(0, CHUNKS, take_b1, 0)

    def product_out(r, _):
        wait(a1r, r, 1)
        widen(a1r, r)

        def one(c, _):
            rows_into(am, r, c)
            rows = pl.ds(pl.multiple_of(r * 64, 64), 64)
            rows_out(dot(am[c, rows, :], bm[c], 1, 1), c)
            return 0

        lax.fori_loop(0, CG, one, 0)
        flush(x1s, r)
        send(x1s, x1r, r, 2)
        return 0

    lax.fori_loop(0, CHUNKS, product_out, 0)

    def columns_of(t0, t1):
        lo = low(CH)
        return jnp.where(lo, t0, swap(t1)), jnp.where(lo, swap(t0), t1)

    def middle(r, _):
        wait(x1r, r, 2)
        for mm in (0, 1):
            m = 2 * r + mm
            at = slice(W * mm, W * mm + W)
            xhat, _ = norm_stats(x1r[r, :, :, at].astype(f32).reshape(CH, W))
            y = (xhat * cols[:, 3:4]).astype(bf16)
            md = (start[m] + gate[m] * dot(wt_of[...], y, 1, 0)).astype(bf16)
            mid[m] = md
            zhat, _ = norm_stats(md.astype(f32))
            normed = (zhat * cols[:, 4:5]).astype(bf16)
            nrm[m] = normed
            p = dot(wt_in[...], normed, 1, 0)
            pm = pair_mask(m)
            b2s[r, :, :, at] = blocks(pm * sig(p[256:384]) * p[384:512])
            a = pm * sig(p[0:128]) * p[128:256]
            q0, q1 = columns_of(a[:, 0:128], a[:, 128:256])
            tile = pl.ds(pl.multiple_of(m * 128, 128), 128)
            a2s[0, :, :, tile] = blocks(q0)
            a2s[1, :, :, tile] = blocks(q1)
            a2s[2, :, :, tile] = blocks(a[:, 256:384])
        send(b2s, b2r, r, 3)
        return 0

    lax.fori_loop(0, CHUNKS, middle, 0)
    send_all(a2s, a2r, 4)

    def take_b2(r, _):
        wait(b2r, r, 3)
        take_rows(b2r, r, b2)
        return 0

    lax.fori_loop(0, CHUNKS, take_b2, 0)

    def product_in(q, _):
        wait(a2r, q, 4)
        widen(a2r, q)

        def one(c, _):
            pick = pl.ds(c, DEV, stride=CG)
            lo = low(DEV)
            for m in range(2 * CHUNKS):
                t = wide[m, pick, :]
                aq[q, c, 32 * m : 32 * m + 16, :] = jnp.where(lo, t, 0.0).astype(bf16)
                aq[q, c, 32 * m + 16 : 32 * m + 32, :] = jnp.where(lo, swap(t), 0.0).astype(bf16)
            rows_out(dot(aq[q, c], b2[c], 0, 0), c)
            return 0

        lax.fori_loop(0, CG, one, 0)
        flush(x2s, q)
        send(x2s, x2r, q, 5)
        return 0

    lax.fori_loop(0, CHUNKS, product_in, 0)

    acc_gate[...] = jnp.zeros_like(acc_gate)
    acc_final[...] = jnp.zeros_like(acc_final)
    acc_mid[...] = jnp.zeros_like(acc_mid)
    acc_proj[...] = jnp.zeros_like(acc_proj)
    acc_norm[...] = jnp.zeros_like(acc_norm)

    def values(r, _):
        wait(x2r, r, 5)
        for mm in (0, 1):
            m = 2 * r + mm
            at = slice(W * mm, W * mm + W)
            xhat, rstd = norm_stats(x2r[r, :, :, at].astype(f32).reshape(CH, W))
            gain = cols[:, 5:6]
            y = (xhat * gain).astype(bf16)
            normed = nrm[m]
            ct = cott[m].astype(f32)
            s = sig(dot(wt_ig[...], normed, 1, 0))
            value = dot(wt_if[...], y, 1, 0)
            gv = (ct * s).astype(bf16)
            gy = dot(w_if[...], gv, 1, 0)
            gx = norm_grad(gy * gain, xhat, rstd)
            gxs[r, :, :, at] = blocks(gx)
            glm = (ct * value * s * (1.0 - s)).astype(bf16)
            gl[m] = glm
            acc_final[...] += dot(y, gv, 1, 1)
            acc_gate[...] += dot(normed, glm, 1, 1)
            acc_mid[...] += lane_sum(gy * xhat)
        send(gxs, gxr, r, 6)
        return 0

    lax.fori_loop(0, CHUNKS, values, 0)
    p1s[0, :, :, 0:128] = blocks(acc_gate[...] * INV)
    p1s[0, :, :, 128:256] = blocks(acc_final[...] * INV)
    send(p1s, p1r, 0, 9)

    def grad_a(q, _):
        wait(gxr, q, 6)
        widen(gxr, q)

        def one(c, _):
            def put(row, head, tail):
                gq[q, c, row : row + 16, 0:128] = head.astype(bf16)
                gq[q, c, row : row + 16, 128:256] = tail.astype(bf16)

            fill_rows(c, put)
            res = dot(b2[c], gq[q, c], 1, 1)
            pick = pl.ds(c, DEV, stride=CG)
            lo = low(DEV)
            for m in range(2 * CHUNKS):
                back[m, pick, :] = jnp.where(
                    lo, res[32 * m : 32 * m + 16], swap(res[32 * m + 16 : 32 * m + 32])
                )
            return 0

        lax.fori_loop(0, CG, one, 0)
        flush(gas, q)
        send(gas, gar, q, 7)
        return 0

    lax.fori_loop(0, CHUNKS, grad_a, 0)

    def grad_b(r, _):
        rows = pl.ds(pl.multiple_of(r * 64, 64), 64)

        def one(c, _):
            res = dot(aq[0, c, rows, :], gq[0, c], 1, 0)
            for q in (1, 2):
                res = res + dot(aq[q, c, rows, :], gq[q, c], 1, 0)
            rows_out(res, c)
            return 0

        lax.fori_loop(0, CG, one, 0)
        flush(gbs, r)
        send(gbs, gbr, r, 8)
        return 0

    lax.fori_loop(0, CHUNKS, grad_b, 0)

    wait(p1r, 0, 9)
    total = p1r[0, 0].astype(f32)
    for s in range(1, DEV):
        total = total + p1r[0, s].astype(f32)
    g1s[...] = total.astype(bf16)
    share(g1s, g1r, 11)

    def wait_ga(q, _):
        wait(gar, q, 7)
        return 0

    lax.fori_loop(0, CHUNKS, wait_ga, 0)

    def finish(r, _):
        wait(gbr, r, 8)
        for mm in (0, 1):
            m = 2 * r + mm
            at = slice(W * mm, W * mm + W)
            normed = nrm[m]
            p = dot(wt_in[...], normed, 1, 0)
            pm = pair_mask(m)
            gb = gbr[r, :, :, at].astype(f32).reshape(CH, W) * pm
            tile = pl.ds(pl.multiple_of(m * 128, 128), 128)
            q0 = gar[0, :, :, tile].astype(f32).reshape(CH, 128)
            q1 = gar[1, :, :, tile].astype(f32).reshape(CH, 128)
            q2 = gar[2, :, :, tile].astype(f32).reshape(CH, 128)
            t0, t1 = columns_of(q0, q1)
            ga = jnp.concatenate([t0, t1, q2], axis=1) * pm
            sa = sig(p[0:128])
            sb = sig(p[256:384])
            gp = jnp.concatenate(
                [
                    ga * p[128:256] * sa * (1.0 - sa),
                    ga * sa,
                    gb * p[384:512] * sb * (1.0 - sb),
                    gb * sb,
                ],
                axis=0,
            ).astype(bf16)
            acc_proj[...] += dot(normed, gp, 1, 1)
            gn = dot(w_in[...], gp, 1, 0) + dot(w_ig[...], gl[m], 1, 0)
            zhat, rstd = norm_stats(mid[m].astype(f32))
            acc_norm[...] += lane_sum(gn * zhat)
            gz = norm_grad(gn * cols[:, 4:5], zhat, rstd)
            res = (cott[m].astype(f32) + gz).astype(bf16)
            out[pl.ds(2 * m, 2)] = dot(sel[...], res, 1, 1).astype(bf16).reshape(2, RES, CH)
        return 0

    lax.fori_loop(0, CHUNKS, finish, 0)

    p2s[0, :, :, 0:512] = blocks(acc_proj[...] * INV)
    gains = jnp.concatenate(
        [
            jnp.sum(acc_norm[...].T, axis=0, keepdims=True),
            jnp.sum(acc_mid[...].T, axis=0, keepdims=True),
            jnp.zeros((CG - 2, 128), f32),
        ],
        axis=0,
    )
    p2s[0, :, :, 512:640] = jnp.broadcast_to((gains * INV)[None], (DEV, CG, 128)).astype(bf16)
    send(p2s, p2r, 0, 10)
    wait(p2r, 0, 10)
    total = p2r[0, 0].astype(f32)
    for s in range(1, DEV):
        total = total + p2r[0, s].astype(f32)
    o_norm[...] = total[0:1, 512:640]
    o_mid[...] = total[1:2, 512:640]
    g2s[...] = total[:, 0:512].astype(bf16)
    share(g2s, g2r, 12)

    for ident, ref in ((11, g1r), (12, g2r)):
        got = ref.at[pl.ds(0, DEV - 1)]
        pltpu.make_async_copy(got, got, recv_sem.at[ident, 0]).wait()
    o_proj[...] = g2r[...].astype(f32).reshape(CH, 512)
    both = g1r[...].astype(f32).reshape(CH, 256)
    o_gate[...] = both[:, 0:128]
    o_final[...] = both[:, 128:256]

    for ident, ref in (
        (0, b1s), (1, a1s), (2, x1s), (3, b2s), (4, a2s), (5, x2s), (6, gxs), (7, gas), (8, gbs),
    ):
        for r in range(CHUNKS):
            sent = ref.at[r, pl.ds(0, DEV - 1)]
            pltpu.make_async_copy(sent, sent, send_sem.at[ident, r]).wait()
    for ident, ref in ((9, p1s), (10, p2s)):
        sent = ref.at[0, pl.ds(0, DEV - 1)]
        pltpu.make_async_copy(sent, sent, send_sem.at[ident, 0]).wait()
    for ident, ref in ((11, g1r), (12, g2r)):
        sent = ref.at[pl.ds(0, DEV - 1)]
        pltpu.make_async_copy(sent, sent, send_sem.at[ident, 0]).wait()


def shards(
    pair, cotangent, residue_mask, chain_ids, chain_embed, out_norm_gain, out_proj, out_gate,
    out_mid_gain, out_final, in_norm_gain, in_proj, in_gate, in_mid_gain, in_final,
):
    vm = pl.BlockSpec(memory_space=pltpu.VMEM)
    sm = pl.BlockSpec(memory_space=pltpu.SMEM)
    v = pltpu.VMEM
    wire = v((CHUNKS, DEV, CG, LANES), bf16)
    steps = lambda dtype: v((2 * CHUNKS, CH, W), dtype)
    part1, part2 = v((1, DEV, CG, 256), bf16), v((1, DEV, CG, 640), bf16)
    square = v((CH, CH), bf16)
    scratch = (
        [v((W, W), bf16), v((CH, 128), f32), v((CH, 128), f32)]
        + [v((4 * CH, CH), bf16), square, square, v((4 * CH, CH), bf16), square, square]
        + [steps(f32), steps(f32), steps(bf16), steps(bf16), steps(bf16), steps(bf16)]
        + [wire] * 9 + [part1, part2, v((CG, 256), bf16), v((CG, 512), bf16)]
        + [wire] * 9 + [part1, part2, v((DEV, CG, 256), bf16), v((DEV, CG, 512), bf16)]
        + [v((LANES // 128, CH, 128), f32)] * 2
        + [v((CG, RES, 256), bf16), v((CG, 256, 256), bf16)]
        + [v((CHUNKS, CG, RES, 128), bf16), v((CG, RES, 256), bf16), v((CHUNKS, CG, 128, 256), bf16)]
        + [v((CH, 512), f32)] + [v((CH, CH), f32)] * 4
        + [pltpu.SemaphoreType.DMA((13, CHUNKS))] * 2
    )
    mask = residue_mask.reshape(1, RES)
    chain = chain_ids.reshape(1, RES)
    gains = [g.reshape(1, CH) for g in (out_norm_gain, out_mid_gain, in_norm_gain, in_mid_gain)]
    outs = [
        jax.ShapeDtypeStruct((ROWS, RES, CH), bf16),
        jax.ShapeDtypeStruct((CH, 512), f32),
        jax.ShapeDtypeStruct((CH, CH), f32),
        jax.ShapeDtypeStruct((CH, CH), f32),
        jax.ShapeDtypeStruct((1, CH), f32),
        jax.ShapeDtypeStruct((1, CH), f32),
    ]
    got = pl.pallas_call(
        kernel,
        out_shape=outs,
        in_specs=[vm] * 4 + [sm] * 2 + [vm] * 11,
        out_specs=[vm] * 6,
        scratch_shapes=scratch,
        compiler_params=pltpu.CompilerParams(
            vmem_limit_bytes=60 * 1024 * 1024, collective_id=0, has_side_effects=True
        ),
    )(
        pair, cotangent, mask, chain, mask, chain, chain_embed, *gains,
        out_proj, out_gate, out_final, in_proj, in_gate, in_final,
    )
    return (*got[:4], got[4].reshape(CH), got[5].reshape(CH))


def solution(mesh):
    whole = P()
    placed = (P("dap", "cplx", None), P("dap", "cplx", None), P("cplx"), P("cplx")) + (whole,) * 11
    return jax.shard_map(
        shards,
        mesh=mesh,
        in_specs=placed,
        out_specs=(
            P("dap", "cplx", None),
            P("cplx", None),
            P("cplx", None),
            P("cplx", None),
            P("cplx"),
            P("cplx"),
        ),
        check_vma=False,
    )
```

time: 933 us -> 150 us (0.16)
  waiting for transfers between devices: 758 us -> 0 us
  Pallas kernels: 0 us -> 143 us
  local copies, waits for them, and re-layouts: 78.5 us -> 5.5 us
  matrix products: 49.2 us -> 0 us
  other arithmetic: 26.1 us -> 0 us
  between operations: 14.2 us -> 0.66 us
    all_gather x3 -> x0, waiting for transfers between devices: 566 us -> none  [the longest x1 205 us: shards(): lax.all_gather(right_b, 'dap', axis=0, tiled=True)]
    psum x1 -> x0, waiting for transfers between devices: 150 us -> none  [together(): subtotal = lax.psum(jnp.concatenate([a.ravel() for a in arrays]), axis)]
    pallas_call x0 -> x1, Pallas kernels: none -> 143 us  [shards(): pl.pallas_call(kernel, out_shape=outs, in_specs=[vm] * 4 + [sm] * 2 + [vm...]
    all_gather x3 -> x0, local copies, waits for them, and re-layouts: 52.2 us -> none  [the longest x1 17.4 us: shards(): shard_rows = lax.all_gather(grad_x_b, 'dap', axis=0, tiled=True)]
    dot_general x16 -> x0, matrix products: 49.2 us -> none  [the longest x1 9.51 us: shards(): jnp.einsum('kjc,ijc->kic', right_ib, shard_rows, preferred_element_type=f32)]
    all_to_all x1 -> x0, waiting for transfers between devices: 41.9 us -> none  [shards(): lax.all_to_all(left_ib, 'dap', split_axis=1, concat_axis=0, tiled=True)]
    convert_element_type x11 -> x0, other arithmetic: 12.2 us -> none  [the longest x3 3.61 us: shards(): part.astype(jnp.float32)]
  transfers between devices with their start and end apart: 5 -> 0, of which waited for: 5 -> 0; matrix products, arithmetic and copies ran while one was open for 2% -> 0% of each run, Pallas kernels for 0% -> 0%
where the time goes in v2:
time: 150 us; the launch traced here: 149 us
  Pallas kernels  143 us (95%)
  local copies, waits for them, and re-layouts  5.5 us (4%)
    pallas_call x1, Pallas kernels, shards(): pl.pallas_call(kernel, out_shape=outs, in_specs=[vm] * 4 + [sm] * 2 + [vm...  143 us
    unnamed x16, local copies, waits for them, and re-layouts  5.5 us

profile of v2, /device:TPU:16, one launch (start us, length us, event | category | flops | bytes accessed | tf_op | source)
XLA Modules:
  0.0 149.3 jit_solution(10276494549585456760)
XLA Ops:
  0.6 143.1 %shard_map.190 = (bf16[12,192,128]{2,1,0:T(8,128)(2,1)}, f32[128,512]{1,0:T(8,128)}, f32[128,128]{1,0:T(8,128)}, f32[128,128]{1,0:T(8,128)}, f32[1,128]{1,0:T(1,128)}, /*index=5*/f32[1,128]{1,0:T(1,128)}) custom-call(bf16[12,192,128]{2,1,0:T(8,128)(2,1)} %pair.1, bf16[12,192,128]{2,1,0:T(8,128)(2,1)} %cot.1, s32[1,192]{1,0:T(1,128)} %bitcast.8, ...), custom_call_target="tpu_custom_call" | custom-call | tf_op jit(solution)/shard_map/pallas_call | solution.py:547
  143.8 0.0 copy-start
  143.8 2.0 %copy.27 = bf16[12,192,128]{2,1,0:T(8,128)(2,1)} copy(bf16[12,192,128]{2,1,0:T(8,128)(2,1)} %get-tuple-element.24) | data formatting | bytes 1179648
  145.8 0.0 copy-done
  145.8 0.0 copy-start.2
  145.8 0.7 copy.28
  146.5 0.2 copy-done.2
  146.6 0.0 copy-start.1
  146.6 0.6 copy.29
  147.3 0.2 copy-done.1
  147.5 0.0 copy-start.4
  147.5 0.6 copy.30
  148.1 0.0 copy-done.4
  148.1 0.0 copy-start.3
  148.1 0.5 copy.31
  148.6 0.2 copy-done.3
  148.8 0.5 copy.32
Async XLA Ops:
  143.8 2.0 %copy-start = (f32[128,512]{1,0:T(8,128)S(1)}, f32[128,512]{1,0:T(8,128)}, u32[]{:S(2)}) copy-start(f32[128,512]{1,0:T(8,128)} %get-tuple-element.25) | copy-start | bytes 786436
  145.8 0.9 copy-start.2
  146.6 0.9 copy-start.1
  147.5 0.6 copy-start.4
  148.1 0.7 copy-start.3

commit v3 on v2

--- a/solution.py
+++ b/solution.py
@@ -10,6 +10,8 @@
 
 ROWS, RES, CH, DEV = 12, 192, 128, 16
 CG = CH // DEV
+HDEV = DEV // 2
+HG = CH // HDEV
 W = 2 * RES
 CHUNKS = 3
 LANES = 2 * W
@@ -73,15 +75,17 @@
 
 
 def kernel(
-    pair, cot, mask_row, chain_row, mask_s, chain_s, embed, gain0, gain1, gain2, gain3,
-    w_out, w_og, w_of, w_in, w_ig, w_if,
-    out, o_proj, o_gate, o_final, o_norm, o_mid,
+    pair_h, cot_h, mask_h, chain_h, embed_h, gain0_h, gain1_h, gain2_h, gain3_h,
+    w_out_h, w_og_h, w_of_h, w_in_h, w_ig_h, w_if_h,
+    out, o_all,
+    pair, cot, mask_row, chain_row, embed, gain0, gain1, gain2, gain3,
+    w_out, w_og, w_of, w_in, w_ig, w_if, mask_s, chain_s, outv, gps,
     sel, vecs, cols, wt_out, wt_og, wt_of, wt_in, wt_ig, wt_if,
     start, gate, mid, nrm, gl, cott,
     b1s, a1s, x1s, b2s, a2s, x2s, gxs, gas, gbs, p1s, p2s, g1s, g2s,
     b1r, a1r, x1r, b2r, a2r, x2r, gxr, gar, gbr, p1r, p2r, g1r, g2r,
-    wide, back, am, bm, aq, b2, gq, acc_proj, acc_gate, acc_final, acc_norm, acc_mid,
-    send_sem, recv_sem,
+    wide, back, bm, aq, b2, gq, acc_proj, acc_gate, acc_final, acc_norm, acc_mid,
+    send_sem, recv_sem, load_sem, out_sem,
 ):
     me = lax.axis_index("dap")
     mx, mz = me // 4, me % 4
@@ -90,6 +94,15 @@
         o = 15 - i
         return ((mx + o % 4) % 4) * 4 + (mz + o // 4) % 4
 
+    mine = mx * 2 + mz % 2
+
+    def seat(to):
+        return (to // 4) * 2 + to % 2
+
+    def near(i):
+        o = HDEV - 1 - i
+        return ((mx + o % 4) % 4) * 4 + (mz // 2) * 2 + (mz + o // 4) % 2
+
     barrier = pltpu.get_barrier_semaphore()
 
     def greet(i, _):
@@ -97,6 +110,21 @@
         return 0
 
     lax.fori_loop(0, DEV - 1, greet, 0)
+
+    loads = [
+        pltpu.make_async_copy(src, dst, load_sem.at[i])
+        for i, (src, dst) in enumerate(
+            (
+                (embed_h, embed), (gain0_h, gain0), (gain1_h, gain1), (gain2_h, gain2),
+                (gain3_h, gain3), (w_og_h, w_og), (w_out_h, w_out),
+                (mask_h, mask_row), (chain_h, chain_row), (mask_h, mask_s), (chain_h, chain_s),
+                (pair_h, pair), (cot_h, cot),
+                (w_of_h, w_of), (w_in_h, w_in), (w_ig_h, w_ig), (w_if_h, w_if),
+            )
+        )
+    ]
+    for load in loads:
+        load.start()
 
     def send(src, dst, r, ident):
         def one(i, _):
@@ -114,6 +142,22 @@
         lax.fori_loop(0, DEV - 1, one, 0)
         dst[r, me] = src[r, me]
 
+    def send_half(src, dst, r, ident, count, partner, slot):
+        def one(i, _):
+            to = partner(i)
+            pltpu.make_async_remote_copy(
+                src_ref=src.at[r, seat(to)],
+                dst_ref=dst.at[r, slot],
+                send_sem=send_sem.at[ident, r],
+                recv_sem=recv_sem.at[ident, r],
+                device_id={"dap": to},
+                device_id_type=MESH,
+            ).start()
+            return 0
+
+        lax.fori_loop(0, count, one, 0)
+        dst[r, slot] = src[r, mine]
+
     def share(src, dst, ident):
         def one(i, _):
             pltpu.make_async_remote_copy(
@@ -130,11 +174,13 @@
         dst[me] = src[...]
 
     def wait(dst, r, ident):
-        blocks = dst.at[r, pl.ds(0, DEV - 1)]
+        blocks = dst.at[r, pl.ds(0, dst.shape[1] - 1)]
         pltpu.make_async_copy(blocks, blocks, recv_sem.at[ident, r]).wait()
 
     sel[...] = selector()
     vecs[...] = jnp.zeros_like(vecs)
+    for load in loads[:11]:
+        load.wait()
     vecs[0:2, :] = embed[...]
     vecs[2:3, :] = gain0[...]
     vecs[3:4, :] = gain1[...]
@@ -167,7 +213,10 @@
     def blocks(v):
         return v.reshape(DEV, CG, v.shape[1]).astype(bf16)
 
-    pl.semaphore_wait(barrier, DEV - 1)
+    def half_blocks(v):
+        return v.reshape(HDEV, HG, v.shape[1]).astype(bf16)
+
+    loads[11].wait()
 
     def project(r, _):
         for mm in (0, 1):
@@ -180,23 +229,31 @@
             normed = (xhat * cols[:, 2:3]).astype(bf16)
             p = dot(wt_out[...], normed, 1, 0)
             pm = pair_mask(m)
-            b1s[r, :, :, at] = blocks(pm * sig(p[256:384]) * p[384:512])
-            a1s[r, :, :, at] = blocks(pm * sig(p[0:128]) * p[128:256])
+            b1s[r, :, :, at] = half_blocks(pm * sig(p[256:384]) * p[384:512])
+            a1s[r, :, :, at] = half_blocks(pm * sig(p[0:128]) * p[128:256])
             gate[m] = sig(dot(wt_og[...], normed, 1, 0))
-        send(b1s, b1r, r, 0)
         return 0
 
     lax.fori_loop(0, CHUNKS, project, 0)
-
-    def send_all(src, dst, ident):
-        def one(r, _):
-            send(src, dst, r, ident)
-            return 0
-
-        lax.fori_loop(0, CHUNKS, one, 0)
-
-    send_all(a1s, a1r, 1)
-
+    pl.semaphore_wait(barrier, DEV - 1)
+
+    def send_b1(r, _):
+        send_half(b1s, b1r, r, 0, DEV - 1, peer, me)
+        return 0
+
+    def send_a1(r, _):
+        send_half(a1s, a1r, r, 1, HDEV - 1, near, mine)
+        return 0
+
+    def sent(ref, r, ident):
+        blocks_out = ref.at[r, pl.ds(0, ref.shape[1] - 1)]
+        pltpu.make_async_copy(blocks_out, blocks_out, send_sem.at[ident, r]).wait()
+
+    lax.fori_loop(0, CHUNKS, send_b1, 0)
+    send_a1(0, 0)
+
+    for load in loads[12:]:
+        load.wait()
     for t in range(4):
         wt_in[128 * t : 128 * t + 128, :] = turn(w_in[:, 128 * t : 128 * t + 128])
     wt_of[...] = turn(w_of[...])
@@ -208,22 +265,31 @@
         return 0
 
     lax.fori_loop(0, 2 * CHUNKS, turn_cot, 0)
-    bm[:, RES:256, :] = jnp.zeros((CG, 256 - RES, 256), bf16)
-    gq[...] = jnp.zeros_like(gq)
+    bm[:, RES:256, :] = jnp.zeros((HG, 256 - RES, 256), bf16)
+
+    def channels(count, body, width=4):
+        def group(g, _):
+            for u in range(width):
+                body(g * width + u)
+            return 0
+
+        lax.fori_loop(0, count // width, group, 0)
 
     def widen(src, r):
+        rows = src.shape[1] * src.shape[2]
         for t in range(LANES // 128):
-            wide[t] = src[r, :, :, 128 * t : 128 * t + 128].astype(f32).reshape(CH, 128)
-
-    def fill_rows(c, put):
-        pick = pl.ds(c, DEV, stride=CG)
+            tile = src[r, :, :, 128 * t : 128 * t + 128].astype(f32)
+            wide[t, 0:rows, :] = tile.reshape(rows, 128)
+
+    def fill_rows(c, put, stride=CG):
+        pick = pl.ds(c, DEV, stride=stride)
         lo = low(DEV)
         for mm in (0, 1):
             tail = wide[3 * mm + 2, pick, :]
             put(32 * mm, wide[3 * mm, pick, :], jnp.where(lo, tail, 0.0))
             put(32 * mm + 16, wide[3 * mm + 1, pick, :], jnp.where(lo, swap(tail), 0.0))
 
-    def rows_into(mat, r, c):
+    def rows_into(mat, r, c, stride):
         base = r * 64
 
         def put(row, head, tail):
@@ -231,16 +297,13 @@
             mat[c, at, 0:128] = head.astype(bf16)
             mat[c, at, 128:256] = tail.astype(bf16)
 
-        fill_rows(c, put)
+        fill_rows(c, put, stride)
 
     def take_rows(src, r, mat):
         widen(src, r)
-
-        def one(c, _):
-            rows_into(mat, r, c)
-            return 0
-
-        lax.fori_loop(0, CG, one, 0)
+        count = src.shape[2]
+
+        channels(count, lambda c: rows_into(mat, r, c, count))
 
     def rows_out(res, c):
         pick = pl.ds(c, DEV, stride=CG)
@@ -255,28 +318,46 @@
 
     def flush(dst, r):
         for t in range(LANES // 128):
-            dst[r, :, :, 128 * t : 128 * t + 128] = back[t].reshape(DEV, CG, 128).astype(bf16)
-
-    def take_b1(r, _):
+            tile = back[t].reshape(dst.shape[1], dst.shape[2], 128)
+            dst[r, :, :, 128 * t : 128 * t + 128] = tile.astype(bf16)
+
+    def take_b1(r):
         wait(b1r, r, 0)
         take_rows(b1r, r, bm)
-        return 0
-
-    lax.fori_loop(0, CHUNKS, take_b1, 0)
+
+    take_b1(0)
+    lax.fori_loop(1, CHUNKS, send_a1, 0)
+    take_b1(1)
+    take_b1(2)
 
     def product_out(r, _):
         wait(a1r, r, 1)
         widen(a1r, r)
 
-        def one(c, _):
-            rows_into(am, r, c)
-            rows = pl.ds(pl.multiple_of(r * 64, 64), 64)
-            rows_out(dot(am[c, rows, :], bm[c], 1, 1), c)
-            return 0
-
-        lax.fori_loop(0, CG, one, 0)
+        def one(c):
+            pick = pl.ds(c, HDEV, stride=HG)
+            lo = low(HDEV)
+            parts = []
+            for mm in (0, 1):
+                tail = wide[3 * mm + 2, pick, :]
+                heads = jnp.concatenate([wide[3 * mm, pick, :], wide[3 * mm + 1, pick, :]], axis=0)
+                tails = jnp.concatenate(
+                    [jnp.where(lo, tail, 0.0), jnp.where(lo, swap(tail), 0.0)], axis=0
+                )
+                parts.append(jnp.concatenate([heads, tails], axis=1))
+            rows = jnp.concatenate(parts, axis=0).astype(bf16)
+            res = dot(rows, bm[c], 1, 1)
+            for mm in (0, 1):
+                u = 16 * mm
+                back[3 * mm, pick, :] = res[u : u + 8, 0:128]
+                back[3 * mm + 1, pick, :] = res[u + 8 : u + 16, 0:128]
+                back[3 * mm + 2, pick, :] = jnp.where(
+                    lo, res[u : u + 8, 128:256], swap(res[u + 8 : u + 16, 128:256])
+                )
+
+        channels(HG, one)
         flush(x1s, r)
-        send(x1s, x1r, r, 2)
+        send_half(x1s, x1r, r, 2, HDEV - 1, near, mine)
         return 0
 
     lax.fori_loop(0, CHUNKS, product_out, 0)
@@ -310,30 +391,32 @@
         return 0
 
     lax.fori_loop(0, CHUNKS, middle, 0)
-    send_all(a2s, a2r, 4)
-
-    def take_b2(r, _):
+    send(a2s, a2r, 0, 4)
+
+    for r in range(CHUNKS):
+        if r > 0:
+            sent(b2s, r, 3)
+            send(a2s, a2r, r, 4)
         wait(b2r, r, 3)
         take_rows(b2r, r, b2)
-        return 0
-
-    lax.fori_loop(0, CHUNKS, take_b2, 0)
 
     def product_in(q, _):
         wait(a2r, q, 4)
         widen(a2r, q)
 
-        def one(c, _):
+        def one(c):
             pick = pl.ds(c, DEV, stride=CG)
             lo = low(DEV)
+            parts = []
             for m in range(2 * CHUNKS):
                 t = wide[m, pick, :]
-                aq[q, c, 32 * m : 32 * m + 16, :] = jnp.where(lo, t, 0.0).astype(bf16)
-                aq[q, c, 32 * m + 16 : 32 * m + 32, :] = jnp.where(lo, swap(t), 0.0).astype(bf16)
-            rows_out(dot(aq[q, c], b2[c], 0, 0), c)
-            return 0
-
-        lax.fori_loop(0, CG, one, 0)
+                parts.append(jnp.where(lo, t, 0.0).astype(bf16))
+                parts.append(jnp.where(lo, swap(t), 0.0).astype(bf16))
+            cols_q = jnp.concatenate(parts, axis=0)
+            aq[q, c] = cols_q
+            rows_out(dot(cols_q, b2[c], 0, 0), c)
+
+        channels(CG, one)
         flush(x2s, q)
         send(x2s, x2r, q, 5)
         return 0
@@ -379,44 +462,46 @@
         wait(gxr, q, 6)
         widen(gxr, q)
 
-        def one(c, _):
+        def one(c):
+            parts = []
+
             def put(row, head, tail):
-                gq[q, c, row : row + 16, 0:128] = head.astype(bf16)
-                gq[q, c, row : row + 16, 128:256] = tail.astype(bf16)
+                parts.append(jnp.concatenate([head, tail], axis=1).astype(bf16))
 
             fill_rows(c, put)
-            res = dot(b2[c], gq[q, c], 1, 1)
+            parts.append(jnp.zeros((64, 256), bf16))
+            rows_q = jnp.concatenate(parts, axis=0)
+            gq[q, c] = rows_q
+            res = dot(b2[c], rows_q, 1, 1)
             pick = pl.ds(c, DEV, stride=CG)
             lo = low(DEV)
             for m in range(2 * CHUNKS):
                 back[m, pick, :] = jnp.where(
                     lo, res[32 * m : 32 * m + 16], swap(res[32 * m + 16 : 32 * m + 32])
                 )
-            return 0
-
-        lax.fori_loop(0, CG, one, 0)
+
+        channels(CG, one)
         flush(gas, q)
         send(gas, gar, q, 7)
         return 0
 
     lax.fori_loop(0, CHUNKS, grad_a, 0)
 
-    def grad_b(r, _):
+    def grad_b(r):
         rows = pl.ds(pl.multiple_of(r * 64, 64), 64)
 
-        def one(c, _):
+        def one(c):
             res = dot(aq[0, c, rows, :], gq[0, c], 1, 0)
             for q in (1, 2):
                 res = res + dot(aq[q, c, rows, :], gq[q, c], 1, 0)
             rows_out(res, c)
-            return 0
-
-        lax.fori_loop(0, CG, one, 0)
+
+        channels(CG, one)
         flush(gbs, r)
         send(gbs, gbr, r, 8)
-        return 0
-
-    lax.fori_loop(0, CHUNKS, grad_b, 0)
+
+    for r in range(CHUNKS):
+        grad_b(r)
 
     wait(p1r, 0, 9)
     total = p1r[0, 0].astype(f32)
@@ -457,18 +542,30 @@
                 ],
                 axis=0,
             ).astype(bf16)
+            gps[m] = gp
             acc_proj[...] += dot(normed, gp, 1, 1)
-            gn = dot(w_in[...], gp, 1, 0) + dot(w_ig[...], gl[m], 1, 0)
-            zhat, rstd = norm_stats(mid[m].astype(f32))
-            acc_norm[...] += lane_sum(gn * zhat)
-            gz = norm_grad(gn * cols[:, 4:5], zhat, rstd)
-            res = (cott[m].astype(f32) + gz).astype(bf16)
-            out[pl.ds(2 * m, 2)] = dot(sel[...], res, 1, 1).astype(bf16).reshape(2, RES, CH)
         return 0
 
     lax.fori_loop(0, CHUNKS, finish, 0)
-
-    p2s[0, :, :, 0:512] = blocks(acc_proj[...] * INV)
+    p2s[0] = blocks(acc_proj[...] * INV)
+    send(p2s, p2r, 0, 10)
+
+    def deliver_pair(m):
+        rows = pl.ds(2 * m, 2)
+        return pltpu.make_async_copy(outv.at[rows], out.at[rows], out_sem.at[m])
+
+    def last(m, _):
+        gn = dot(w_in[...], gps[m], 1, 0) + dot(w_ig[...], gl[m], 1, 0)
+        zhat, rstd = norm_stats(mid[m].astype(f32))
+        acc_norm[...] += lane_sum(gn * zhat)
+        gz = norm_grad(gn * cols[:, 4:5], zhat, rstd)
+        res = (cott[m].astype(f32) + gz).astype(bf16)
+        outv[pl.ds(2 * m, 2)] = dot(sel[...], res, 1, 1).astype(bf16).reshape(2, RES, CH)
+        deliver_pair(m).start()
+        return 0
+
+    lax.fori_loop(0, 2 * CHUNKS, last, 0)
+
     gains = jnp.concatenate(
         [
             jnp.sum(acc_norm[...].T, axis=0, keepdims=True),
@@ -477,37 +574,46 @@
         ],
         axis=0,
     )
-    p2s[0, :, :, 512:640] = jnp.broadcast_to((gains * INV)[None], (DEV, CG, 128)).astype(bf16)
-    send(p2s, p2r, 0, 10)
+    g2s[:, 512:640] = (gains * INV).astype(bf16)
     wait(p2r, 0, 10)
     total = p2r[0, 0].astype(f32)
     for s in range(1, DEV):
         total = total + p2r[0, s].astype(f32)
-    o_norm[...] = total[0:1, 512:640]
-    o_mid[...] = total[1:2, 512:640]
-    g2s[...] = total[:, 0:512].astype(bf16)
+    g2s[:, 0:512] = total.astype(bf16)
     share(g2s, g2r, 12)
+    for m in range(2 * CHUNKS):
+        deliver_pair(m).wait()
 
     for ident, ref in ((11, g1r), (12, g2r)):
         got = ref.at[pl.ds(0, DEV - 1)]
         pltpu.make_async_copy(got, got, recv_sem.at[ident, 0]).wait()
-    o_proj[...] = g2r[...].astype(f32).reshape(CH, 512)
-    both = g1r[...].astype(f32).reshape(CH, 256)
-    o_gate[...] = both[:, 0:128]
-    o_final[...] = both[:, 128:256]
-
-    for ident, ref in (
-        (0, b1s), (1, a1s), (2, x1s), (3, b2s), (4, a2s), (5, x2s), (6, gxs), (7, gas), (8, gbs),
+    o_all[0:CH, 0:512] = g2r[:, :, 0:512].astype(f32).reshape(CH, 512)
+    total = g2r[0, :, 512:640].astype(f32)
+    for s in range(1, DEV):
+        total = total + g2r[s, :, 512:640].astype(f32)
+    o_all[CH : CH + CG, 0:128] = total
+    o_all[0:CH, 512:768] = g1r[...].astype(f32).reshape(CH, 256)
+
+    for ident, ref, rest in (
+        (0, b1r, (0, 1, 2)), (1, a1s, (0, 1, 2)), (2, x1s, (0, 1, 2)), (3, b2s, (0,)),
+        (4, a2s, (0, 1, 2)), (5, x2s, (0, 1, 2)), (6, gxs, (0, 1, 2)), (7, gas, (0, 1, 2)),
+        (8, gbs, (0, 1, 2)),
+        (9, p1s, (0,)), (10, p2s, (0,)),
     ):
-        for r in range(CHUNKS):
-            sent = ref.at[r, pl.ds(0, DEV - 1)]
-            pltpu.make_async_copy(sent, sent, send_sem.at[ident, r]).wait()
-    for ident, ref in ((9, p1s), (10, p2s)):
-        sent = ref.at[0, pl.ds(0, DEV - 1)]
-        pltpu.make_async_copy(sent, sent, send_sem.at[ident, 0]).wait()
+        for r in rest:
+            sent(ref, r, ident)
     for ident, ref in ((11, g1r), (12, g2r)):
-        sent = ref.at[pl.ds(0, DEV - 1)]
-        pltpu.make_async_copy(sent, sent, send_sem.at[ident, 0]).wait()
+        gone = ref.at[pl.ds(0, DEV - 1)]
+        pltpu.make_async_copy(gone, gone, send_sem.at[ident, 0]).wait()
+
+
+def deliver(pair_in, all_in, pair_out, proj, gate, final, norm, mid):
+    pair_out[...] = pair_in[...]
+    proj[...] = all_in[0:CH, 0:512]
+    gate[...] = all_in[0:CH, 512:640]
+    final[...] = all_in[0:CH, 640:768]
+    norm[...] = all_in[CH : CH + 1, 0:128]
+    mid[...] = all_in[CH + 1 : CH + 2, 0:128]
 
 
 def shards(
@@ -515,23 +621,30 @@
     out_mid_gain, out_final, in_norm_gain, in_proj, in_gate, in_mid_gain, in_final,
 ):
     vm = pl.BlockSpec(memory_space=pltpu.VMEM)
-    sm = pl.BlockSpec(memory_space=pltpu.SMEM)
+    hbm = pl.BlockSpec(memory_space=pl.ANY)
     v = pltpu.VMEM
     wire = v((CHUNKS, DEV, CG, LANES), bf16)
+    half = v((CHUNKS, HDEV, HG, LANES), bf16)
+    twice = v((CHUNKS, DEV, HG, LANES), bf16)
     steps = lambda dtype: v((2 * CHUNKS, CH, W), dtype)
-    part1, part2 = v((1, DEV, CG, 256), bf16), v((1, DEV, CG, 640), bf16)
+    part1, part2 = v((1, DEV, CG, 256), bf16), v((1, DEV, CG, 512), bf16)
     square = v((CH, CH), bf16)
+    block = v((ROWS, RES, CH), bf16)
     scratch = (
-        [v((W, W), bf16), v((CH, 128), f32), v((CH, 128), f32)]
+        [block, block] + [v((1, RES), jnp.int32)] * 2 + [v((2, CH), f32)] + [v((1, CH), f32)] * 4
+        + [v((CH, 512), bf16), square, square, v((CH, 512), bf16), square, square]
+        + [pltpu.SMEM((1, RES), jnp.int32)] * 2 + [block, v((2 * CHUNKS, 4 * CH, W), bf16)]
+        + [v((W, W), bf16), v((CH, 128), f32), v((CH, 128), f32)]
         + [v((4 * CH, CH), bf16), square, square, v((4 * CH, CH), bf16), square, square]
         + [steps(f32), steps(f32), steps(bf16), steps(bf16), steps(bf16), steps(bf16)]
-        + [wire] * 9 + [part1, part2, v((CG, 256), bf16), v((CG, 512), bf16)]
-        + [wire] * 9 + [part1, part2, v((DEV, CG, 256), bf16), v((DEV, CG, 512), bf16)]
-        + [v((LANES // 128, CH, 128), f32)] * 2
-        + [v((CG, RES, 256), bf16), v((CG, 256, 256), bf16)]
+        + [half] * 3 + [wire] * 6 + [part1, part2, v((CG, 256), bf16), v((CG, 640), bf16)]
+        + [twice, half, half] + [wire] * 6 + [part1, part2, v((DEV, CG, 256), bf16), v((DEV, CG, 640), bf16)]
+        + [v((LANES // 128, DEV * HG, 128), f32), v((LANES // 128, CH, 128), f32)]
+        + [v((HG, 256, 256), bf16)]
         + [v((CHUNKS, CG, RES, 128), bf16), v((CG, RES, 256), bf16), v((CHUNKS, CG, 128, 256), bf16)]
         + [v((CH, 512), f32)] + [v((CH, CH), f32)] * 4
         + [pltpu.SemaphoreType.DMA((13, CHUNKS))] * 2
+        + [pltpu.SemaphoreType.DMA((17,)), pltpu.SemaphoreType.DMA((2 * CHUNKS,))]
     )
     mask = residue_mask.reshape(1, RES)
     chain = chain_ids.reshape(1, RES)
@@ -544,19 +657,21 @@
         jax.ShapeDtypeStruct((1, CH), f32),
         jax.ShapeDtypeStruct((1, CH), f32),
     ]
+    params = pltpu.CompilerParams(
+        vmem_limit_bytes=60 * 1024 * 1024, collective_id=0, has_side_effects=True
+    )
     got = pl.pallas_call(
         kernel,
-        out_shape=outs,
-        in_specs=[vm] * 4 + [sm] * 2 + [vm] * 11,
-        out_specs=[vm] * 6,
+        out_shape=[outs[0], jax.ShapeDtypeStruct((CH + CG, 768), f32)],
+        in_specs=[hbm] * 15,
+        out_specs=[hbm, vm],
         scratch_shapes=scratch,
-        compiler_params=pltpu.CompilerParams(
-            vmem_limit_bytes=60 * 1024 * 1024, collective_id=0, has_side_effects=True
-        ),
+        compiler_params=params,
     )(
-        pair, cotangent, mask, chain, mask, chain, chain_embed, *gains,
+        pair, cotangent, mask, chain, chain_embed, *gains,
         out_proj, out_gate, out_final, in_proj, in_gate, in_final,
     )
+    got = pl.pallas_call(deliver, out_shape=outs, in_specs=[vm] * 2, out_specs=[vm] * 6)(*got)
     return (*got[:4], got[4].reshape(CH), got[5].reshape(CH))
 
 

time: 150 us -> 140 us (0.933)
  local copies, waits for them, and re-layouts: 5.5 us -> 0 us
  Pallas kernels: 143 us -> 138 us
    unnamed x16 -> x0, local copies, waits for them, and re-layouts: 5.5 us -> none
    pallas_call x1 -> x2, Pallas kernels: 143 us -> 138 us  [the longest x1 136 us: shards(): pl.pallas_call(kernel, out_shape=[outs[0], jax.ShapeDtypeStruct((CH + CG,...]
where the time goes in v3:
time: 140 us; the launch traced here: 139 us
  Pallas kernels  138 us (99%)
    pallas_call x1, Pallas kernels, shards(): pl.pallas_call(kernel, out_shape=[outs[0], jax.ShapeDtypeStruct((CH + CG,...  136 us

profile of v3, /device:TPU:16, one launch (start us, length us, event | category | flops | bytes accessed | tf_op | source)
XLA Modules:
  0.0 139.1 jit_solution(17535512703351753106)
XLA Ops:
  0.6 136.3 %shard_map.190 = (bf16[12,192,128]{2,1,0:T(8,128)(2,1)}, f32[136,768]{1,0:T(8,128)}) custom-call(bf16[12,192,128]{2,1,0:T(8,128)(2,1)} %pair_h.1, bf16[12,192,128]{2,1,0:T(8,128)(2,1)} %cot_h.1, s32[1,192]{1,0:T(1,128)} %bitcast.8, s32[1,192]{1,0:T(1,128)} %bitcast.9, f32[2,128]{1,0:T(2,128)} %embed_h.1, f32[1,128]{1,0:T(1,128)} %bitcast.10, ...), custom_call_target="tpu_custom_call" | custom-call | tf_op jit(solution)/shard_map/pallas_call | solution.py:663
  137.0 2.1 %shard_map.191 = (bf16[12,192,128]{2,1,0:T(8,128)(2,1)}, f32[128,512]{1,0:T(8,128)}, f32[128,128]{1,0:T(8,128)}, f32[128,128]{1,0:T(8,128)}, f32[1,128]{1,0:T(1,128)}, /*index=5*/f32[1,128]{1,0:T(1,128)}) custom-call(bf16[12,192,128]{2,1,0:T(8,128)(2,1)} %get-tuple-element.14.pair_in, f32[136,768]{1,0:T(8,128)} %get-tuple-element.15.all_in), custom_call_target="tpu_custom_call" | custom-call | tf_op jit(solution)/shard_map/pallas_call | solution.py:674

commit v4 on v3

--- a/solution.py
+++ b/solution.py
@@ -82,17 +82,19 @@
     w_out, w_og, w_of, w_in, w_ig, w_if, mask_s, chain_s, outv, gps,
     sel, vecs, cols, wt_out, wt_og, wt_of, wt_in, wt_ig, wt_if,
     start, gate, mid, nrm, gl, cott,
-    b1s, a1s, x1s, b2s, a2s, x2s, gxs, gas, gbs, p1s, p2s, g1s, g2s,
-    b1r, a1r, x1r, b2r, a2r, x2r, gxr, gar, gbr, p1r, p2r, g1r, g2r,
-    wide, back, bm, aq, b2, gq, acc_proj, acc_gate, acc_final, acc_norm, acc_mid,
+    b1s, a1s, x1s, b2s, a2s, x2s, gxs, gas, gbs, p1s, p2s, p3s, g1s, g2s, g3s, h1s, h3s,
+    b1r, a1r, x1r, b2r, a2r, x2r, gxr, gar, gbr, p1r, p2r, p3r, g1r, g2r, g3r, h1r, h3r,
+    wide, back, bm, aq, b2, gq, acc_left, acc_right, acc_gate, acc_final, acc_norm, acc_mid,
     send_sem, recv_sem, load_sem, out_sem,
 ):
     me = lax.axis_index("dap")
     mx, mz = me // 4, me % 4
 
     def peer(i):
-        o = 15 - i
-        return ((mx + o % 4) % 4) * 4 + (mz + o // 4) % 4
+        k = i // 4
+        d = 2 + k - (k // 2) * (2 * k - 1)
+        z = (mz // 2 + d // 2) % 2 * 2 + (mz + d) % 2
+        return ((mx + 3 - i % 4) % 4) * 4 + z
 
     mine = mx * 2 + mz % 2
 
@@ -173,6 +175,37 @@
         lax.fori_loop(0, DEV - 1, one, 0)
         dst[me] = src[...]
 
+    def share_half(src, dst, ident):
+        def one(i, _):
+            pltpu.make_async_remote_copy(
+                src_ref=src,
+                dst_ref=dst.at[mine],
+                send_sem=send_sem.at[ident, 0],
+                recv_sem=recv_sem.at[ident, 0],
+                device_id={"dap": near(i)},
+                device_id_type=MESH,
+            ).start()
+            return 0
+
+        lax.fori_loop(0, HDEV - 1, one, 0)
+        dst[mine] = src[...]
+
+    def across(src, dst, ident):
+        return pltpu.make_async_remote_copy(
+            src_ref=src,
+            dst_ref=dst,
+            send_sem=send_sem.at[ident, 0],
+            recv_sem=recv_sem.at[ident, 0],
+            device_id={"dap": mx * 4 + (mz + 2) % 4},
+            device_id_type=MESH,
+        )
+
+    def summed(ref, count):
+        total = ref[0].astype(f32)
+        for k in range(1, count):
+            total = total + ref[k].astype(f32)
+        return total
+
     def wait(dst, r, ident):
         blocks = dst.at[r, pl.ds(0, dst.shape[1] - 1)]
         pltpu.make_async_copy(blocks, blocks, recv_sem.at[ident, r]).wait()
@@ -234,7 +267,7 @@
             gate[m] = sig(dot(wt_og[...], normed, 1, 0))
         return 0
 
-    lax.fori_loop(0, CHUNKS, project, 0)
+    project(0, 0)
     pl.semaphore_wait(barrier, DEV - 1)
 
     def send_b1(r, _):
@@ -249,7 +282,14 @@
         blocks_out = ref.at[r, pl.ds(0, ref.shape[1] - 1)]
         pltpu.make_async_copy(blocks_out, blocks_out, send_sem.at[ident, r]).wait()
 
-    lax.fori_loop(0, CHUNKS, send_b1, 0)
+    send_b1(0, 0)
+
+    def project_and_send(r, _):
+        project(r, 0)
+        send_b1(r, 0)
+        return 0
+
+    lax.fori_loop(1, CHUNKS, project_and_send, 0)
     send_a1(0, 0)
 
     for load in loads[12:]:
@@ -426,7 +466,8 @@
     acc_gate[...] = jnp.zeros_like(acc_gate)
     acc_final[...] = jnp.zeros_like(acc_final)
     acc_mid[...] = jnp.zeros_like(acc_mid)
-    acc_proj[...] = jnp.zeros_like(acc_proj)
+    acc_left[...] = jnp.zeros_like(acc_left)
+    acc_right[...] = jnp.zeros_like(acc_right)
     acc_norm[...] = jnp.zeros_like(acc_norm)
 
     def values(r, _):
@@ -454,9 +495,19 @@
         return 0
 
     lax.fori_loop(0, CHUNKS, values, 0)
-    p1s[0, :, :, 0:128] = blocks(acc_gate[...] * INV)
-    p1s[0, :, :, 128:256] = blocks(acc_final[...] * INV)
-    send(p1s, p1r, 0, 9)
+    p1s[0, :, :, 0:128] = half_blocks(acc_gate[...] * INV)
+    p1s[0, :, :, 128:256] = half_blocks(acc_final[...] * INV)
+    send_half(p1s, p1r, 0, 9, HDEV - 1, near, mine)
+
+    def sum_half(src, half_sum, other, ident, next_ident):
+        wait(src, 0, ident)
+        half_sum[...] = summed(src.at[0], HDEV).astype(bf16)
+        across(half_sum, other, next_ident).start()
+
+    def sum_both(half_sum, other, full, result, ident, next_ident):
+        across(half_sum, other, ident).wait_recv()
+        full[...] = (half_sum[...].astype(f32) + other[...].astype(f32)).astype(bf16)
+        share_half(full, result, next_ident)
 
     def grad_a(q, _):
         wait(gxr, q, 6)
@@ -500,21 +551,35 @@
         flush(gbs, r)
         send(gbs, gbr, r, 8)
 
+    sum_half(p1r, h1s, h1r, 9, 11)
     for r in range(CHUNKS):
         grad_b(r)
-
-    wait(p1r, 0, 9)
-    total = p1r[0, 0].astype(f32)
-    for s in range(1, DEV):
-        total = total + p1r[0, s].astype(f32)
-    g1s[...] = total.astype(bf16)
-    share(g1s, g1r, 11)
+    sum_both(h1s, h1r, g1s, g1r, 11, 12)
 
     def wait_ga(q, _):
         wait(gar, q, 7)
         return 0
 
     lax.fori_loop(0, CHUNKS, wait_ga, 0)
+
+    def left(m, _):
+        normed = nrm[m]
+        p = dot(wt_in[0:256, :], normed, 1, 0)
+        tile = pl.ds(pl.multiple_of(m * 128, 128), 128)
+        q0 = gar[0, :, :, tile].astype(f32).reshape(CH, 128)
+        q1 = gar[1, :, :, tile].astype(f32).reshape(CH, 128)
+        q2 = gar[2, :, :, tile].astype(f32).reshape(CH, 128)
+        t0, t1 = columns_of(q0, q1)
+        ga = jnp.concatenate([t0, t1, q2], axis=1) * pair_mask(m)
+        sa = sig(p[0:128])
+        gp = jnp.concatenate([ga * p[128:256] * sa * (1.0 - sa), ga * sa], axis=0).astype(bf16)
+        gps[m, 0:256, :] = gp
+        acc_left[...] += dot(normed, gp, 1, 1)
+        return 0
+
+    lax.fori_loop(0, 2 * CHUNKS, left, 0)
+    p3s[0] = half_blocks(acc_left[...] * INV)
+    send_half(p3s, p3r, 0, 13, HDEV - 1, near, mine)
 
     def finish(r, _):
         wait(gbr, r, 8)
@@ -522,33 +587,18 @@
             m = 2 * r + mm
             at = slice(W * mm, W * mm + W)
             normed = nrm[m]
-            p = dot(wt_in[...], normed, 1, 0)
-            pm = pair_mask(m)
-            gb = gbr[r, :, :, at].astype(f32).reshape(CH, W) * pm
-            tile = pl.ds(pl.multiple_of(m * 128, 128), 128)
-            q0 = gar[0, :, :, tile].astype(f32).reshape(CH, 128)
-            q1 = gar[1, :, :, tile].astype(f32).reshape(CH, 128)
-            q2 = gar[2, :, :, tile].astype(f32).reshape(CH, 128)
-            t0, t1 = columns_of(q0, q1)
-            ga = jnp.concatenate([t0, t1, q2], axis=1) * pm
-            sa = sig(p[0:128])
-            sb = sig(p[256:384])
-            gp = jnp.concatenate(
-                [
-                    ga * p[128:256] * sa * (1.0 - sa),
-                    ga * sa,
-                    gb * p[384:512] * sb * (1.0 - sb),
-                    gb * sb,
-                ],
-                axis=0,
-            ).astype(bf16)
-            gps[m] = gp
-            acc_proj[...] += dot(normed, gp, 1, 1)
+            p = dot(wt_in[256:512, :], normed, 1, 0)
+            gb = gbr[r, :, :, at].astype(f32).reshape(CH, W) * pair_mask(m)
+            sb = sig(p[0:128])
+            gp = jnp.concatenate([gb * p[128:256] * sb * (1.0 - sb), gb * sb], axis=0).astype(bf16)
+            gps[m, 256:512, :] = gp
+            acc_right[...] += dot(normed, gp, 1, 1)
         return 0
 
     lax.fori_loop(0, CHUNKS, finish, 0)
-    p2s[0] = blocks(acc_proj[...] * INV)
+    p2s[0] = blocks(acc_right[...] * INV)
     send(p2s, p2r, 0, 10)
+    sum_half(p3r, h3s, h3r, 13, 14)
 
     def deliver_pair(m):
         rows = pl.ds(2 * m, 2)
@@ -565,6 +615,7 @@
         return 0
 
     lax.fori_loop(0, 2 * CHUNKS, last, 0)
+    sum_both(h3s, h3r, g3s, g3r, 14, 15)
 
     gains = jnp.concatenate(
         [
@@ -574,37 +625,34 @@
         ],
         axis=0,
     )
-    g2s[:, 512:640] = (gains * INV).astype(bf16)
+    g2s[:, 256:384] = (gains * INV).astype(bf16)
     wait(p2r, 0, 10)
-    total = p2r[0, 0].astype(f32)
-    for s in range(1, DEV):
-        total = total + p2r[0, s].astype(f32)
-    g2s[:, 0:512] = total.astype(bf16)
-    share(g2s, g2r, 12)
+    g2s[:, 0:256] = summed(p2r.at[0], DEV).astype(bf16)
+    share(g2s, g2r, 16)
     for m in range(2 * CHUNKS):
         deliver_pair(m).wait()
 
-    for ident, ref in ((11, g1r), (12, g2r)):
-        got = ref.at[pl.ds(0, DEV - 1)]
+    for ident, ref in ((12, g1r), (15, g3r), (16, g2r)):
+        got = ref.at[pl.ds(0, ref.shape[0] - 1)]
         pltpu.make_async_copy(got, got, recv_sem.at[ident, 0]).wait()
-    o_all[0:CH, 0:512] = g2r[:, :, 0:512].astype(f32).reshape(CH, 512)
-    total = g2r[0, :, 512:640].astype(f32)
-    for s in range(1, DEV):
-        total = total + g2r[s, :, 512:640].astype(f32)
-    o_all[CH : CH + CG, 0:128] = total
+    o_all[0:CH, 0:256] = g3r[...].astype(f32).reshape(CH, 256)
+    o_all[0:CH, 256:512] = g2r[:, :, 0:256].astype(f32).reshape(CH, 256)
     o_all[0:CH, 512:768] = g1r[...].astype(f32).reshape(CH, 256)
+    o_all[CH : CH + CG, 0:128] = summed(g2r.at[:, :, 256:384], DEV)
 
     for ident, ref, rest in (
         (0, b1r, (0, 1, 2)), (1, a1s, (0, 1, 2)), (2, x1s, (0, 1, 2)), (3, b2s, (0,)),
         (4, a2s, (0, 1, 2)), (5, x2s, (0, 1, 2)), (6, gxs, (0, 1, 2)), (7, gas, (0, 1, 2)),
         (8, gbs, (0, 1, 2)),
-        (9, p1s, (0,)), (10, p2s, (0,)),
+        (9, p1s, (0,)), (10, p2s, (0,)), (13, p3s, (0,)),
     ):
         for r in rest:
             sent(ref, r, ident)
-    for ident, ref in ((11, g1r), (12, g2r)):
-        gone = ref.at[pl.ds(0, DEV - 1)]
+    for ident, ref in ((12, g1r), (15, g3r), (16, g2r)):
+        gone = ref.at[pl.ds(0, ref.shape[0] - 1)]
         pltpu.make_async_copy(gone, gone, send_sem.at[ident, 0]).wait()
+    across(h1s, h1r, 11).wait_send()
+    across(h3s, h3r, 14).wait_send()
 
 
 def deliver(pair_in, all_in, pair_out, proj, gate, final, norm, mid):
@@ -627,7 +675,9 @@
     half = v((CHUNKS, HDEV, HG, LANES), bf16)
     twice = v((CHUNKS, DEV, HG, LANES), bf16)
     steps = lambda dtype: v((2 * CHUNKS, CH, W), dtype)
-    part1, part2 = v((1, DEV, CG, 256), bf16), v((1, DEV, CG, 512), bf16)
+    part, part2 = v((1, HDEV, HG, 256), bf16), v((1, DEV, CG, 256), bf16)
+    piece, piece2 = v((HG, 256), bf16), v((CG, 384), bf16)
+    full, full2 = v((HDEV, HG, 256), bf16), v((DEV, CG, 384), bf16)
     square = v((CH, CH), bf16)
     block = v((ROWS, RES, CH), bf16)
     scratch = (
@@ -637,13 +687,13 @@
         + [v((W, W), bf16), v((CH, 128), f32), v((CH, 128), f32)]
         + [v((4 * CH, CH), bf16), square, square, v((4 * CH, CH), bf16), square, square]
         + [steps(f32), steps(f32), steps(bf16), steps(bf16), steps(bf16), steps(bf16)]
-        + [half] * 3 + [wire] * 6 + [part1, part2, v((CG, 256), bf16), v((CG, 640), bf16)]
-        + [twice, half, half] + [wire] * 6 + [part1, part2, v((DEV, CG, 256), bf16), v((DEV, CG, 640), bf16)]
+        + [half] * 3 + [wire] * 6 + [part, part2, part, piece, piece2, piece, piece, piece]
+        + [twice, half, half] + [wire] * 6 + [part, part2, part, full, full2, full, piece, piece]
         + [v((LANES // 128, DEV * HG, 128), f32), v((LANES // 128, CH, 128), f32)]
         + [v((HG, 256, 256), bf16)]
         + [v((CHUNKS, CG, RES, 128), bf16), v((CG, RES, 256), bf16), v((CHUNKS, CG, 128, 256), bf16)]
-        + [v((CH, 512), f32)] + [v((CH, CH), f32)] * 4
-        + [pltpu.SemaphoreType.DMA((13, CHUNKS))] * 2
+        + [v((CH, 256), f32)] * 2 + [v((CH, CH), f32)] * 4
+        + [pltpu.SemaphoreType.DMA((17, CHUNKS))] * 2
         + [pltpu.SemaphoreType.DMA((17,)), pltpu.SemaphoreType.DMA((2 * CHUNKS,))]
     )
     mask = residue_mask.reshape(1, RES)

time: 140 us -> 136 us (0.971)
  Pallas kernels: 138 us -> 135 us
    pallas_call x1, Pallas kernels: 136 us -> 133 us  [shards(): pl.pallas_call(kernel, out_shape=[outs[0], jax.ShapeDtypeStruct((CH + CG,...]
where the time goes in v4:
time: 136 us
  Pallas kernels  135 us (99%)
    pallas_call x1, Pallas kernels, shards(): pl.pallas_call(kernel, out_shape=[outs[0], jax.ShapeDtypeStruct((CH + CG,...  133 us

profile of v4, /device:TPU:16, one launch (start us, length us, event | category | flops | bytes accessed | tf_op | source)
XLA Modules:
  0.0 135.6 jit_solution(2117544509125386797)
XLA Ops:
  0.6 132.9 %shard_map.190 = (bf16[12,192,128]{2,1,0:T(8,128)(2,1)}, f32[136,768]{1,0:T(8,128)}) custom-call(bf16[12,192,128]{2,1,0:T(8,128)(2,1)} %pair_h.1, bf16[12,192,128]{2,1,0:T(8,128)(2,1)} %cot_h.1, s32[1,192]{1,0:T(1,128)} %bitcast.8, s32[1,192]{1,0:T(1,128)} %bitcast.9, f32[2,128]{1,0:T(2,128)} %embed_h.1, f32[1,128]{1,0:T(1,128)} %bitcast.10, ...), custom_call_target="tpu_custom_call" | custom-call | tf_op jit(solution)/shard_map/pallas_call | solution.py:713
  133.5 2.1 %shard_map.191 = (bf16[12,192,128]{2,1,0:T(8,128)(2,1)}, f32[128,512]{1,0:T(8,128)}, f32[128,128]{1,0:T(8,128)}, f32[128,128]{1,0:T(8,128)}, f32[1,128]{1,0:T(1,128)}, /*index=5*/f32[1,128]{1,0:T(1,128)}) custom-call(bf16[12,192,128]{2,1,0:T(8,128)(2,1)} %get-tuple-element.14.pair_in, f32[136,768]{1,0:T(8,128)} %get-tuple-element.15.all_in), custom_call_target="tpu_custom_call" | custom-call | tf_op jit(solution)/shard_map/pallas_call | solution.py:724

commit v5 on v4

--- a/solution.py
+++ b/solution.py
@@ -79,13 +79,13 @@
     w_out_h, w_og_h, w_of_h, w_in_h, w_ig_h, w_if_h,
     out, o_all,
     pair, cot, mask_row, chain_row, embed, gain0, gain1, gain2, gain3,
-    w_out, w_og, w_of, w_in, w_ig, w_if, mask_s, chain_s, outv, gps,
+    w_out, w_og, w_of, w_in, w_ig, w_if, mask_s, chain_s, gps, fac, scale, sums,
     sel, vecs, cols, wt_out, wt_og, wt_of, wt_in, wt_ig, wt_if,
     start, gate, mid, nrm, gl, cott,
-    b1s, a1s, x1s, b2s, a2s, x2s, gxs, gas, gbs, p1s, p2s, p3s, g1s, g2s, g3s, h1s, h3s,
-    b1r, a1r, x1r, b2r, a2r, x2r, gxr, gar, gbr, p1r, p2r, p3r, g1r, g2r, g3r, h1r, h3r,
+    b1s, a1s, x1s, b2s, a2s, x2s, gxs, gas, gbs, p1s, p2s, p3s, g1s, g2s, g3s, g4s, h1s, h3s,
+    b1r, a1r, x1r, b2r, a2r, x2r, gxr, gar, gbr, p1r, p2r, p3r, g1r, g2r, g3r, g4r, h1r, h3r,
     wide, back, bm, aq, b2, gq, acc_left, acc_right, acc_gate, acc_final, acc_norm, acc_mid,
-    send_sem, recv_sem, load_sem, out_sem,
+    send_sem, recv_sem, load_sem,
 ):
     me = lax.axis_index("dap")
     mx, mz = me // 4, me % 4
@@ -551,10 +551,25 @@
         flush(gbs, r)
         send(gbs, gbr, r, 8)
 
-    sum_half(p1r, h1s, h1r, 9, 11)
     for r in range(CHUNKS):
         grad_b(r)
-    sum_both(h1s, h1r, g1s, g1r, 11, 12)
+
+    def prepare(m, _):
+        p = dot(wt_in[...], nrm[m], 1, 0)
+        pm = pair_mask(m)
+        for k in (0, 256):
+            s = sig(p[k : k + 128])
+            fac[m, k : k + 128, :] = pm * p[k + 128 : k + 256] * s * (1.0 - s)
+            fac[m, k + 128 : k + 256, :] = pm * s
+        zhat, rstd = norm_stats(mid[m].astype(f32))
+        start[m] = zhat
+        scale[m] = jnp.broadcast_to(rstd, (CG, W))
+        gate[m] = dot(w_ig[...], gl[m], 1, 0)
+        return 0
+
+    lax.fori_loop(0, 2 * CHUNKS, prepare, 0)
+    sums[1:2, :] = jnp.sum(acc_mid[...].T, axis=0, keepdims=True)
+    sum_half(p1r, h1s, h1r, 9, 11)
 
     def wait_ga(q, _):
         wait(gar, q, 7)
@@ -563,18 +578,15 @@
     lax.fori_loop(0, CHUNKS, wait_ga, 0)
 
     def left(m, _):
-        normed = nrm[m]
-        p = dot(wt_in[0:256, :], normed, 1, 0)
         tile = pl.ds(pl.multiple_of(m * 128, 128), 128)
         q0 = gar[0, :, :, tile].astype(f32).reshape(CH, 128)
         q1 = gar[1, :, :, tile].astype(f32).reshape(CH, 128)
         q2 = gar[2, :, :, tile].astype(f32).reshape(CH, 128)
         t0, t1 = columns_of(q0, q1)
-        ga = jnp.concatenate([t0, t1, q2], axis=1) * pair_mask(m)
-        sa = sig(p[0:128])
-        gp = jnp.concatenate([ga * p[128:256] * sa * (1.0 - sa), ga * sa], axis=0).astype(bf16)
+        ga = jnp.concatenate([t0, t1, q2], axis=1)
+        gp = jnp.concatenate([ga * fac[m, 0:128, :], ga * fac[m, 128:256, :]], axis=0).astype(bf16)
         gps[m, 0:256, :] = gp
-        acc_left[...] += dot(normed, gp, 1, 1)
+        acc_left[...] += dot(nrm[m], gp, 1, 1)
         return 0
 
     lax.fori_loop(0, 2 * CHUNKS, left, 0)
@@ -586,59 +598,47 @@
         for mm in (0, 1):
             m = 2 * r + mm
             at = slice(W * mm, W * mm + W)
-            normed = nrm[m]
-            p = dot(wt_in[256:512, :], normed, 1, 0)
-            gb = gbr[r, :, :, at].astype(f32).reshape(CH, W) * pair_mask(m)
-            sb = sig(p[0:128])
-            gp = jnp.concatenate([gb * p[128:256] * sb * (1.0 - sb), gb * sb], axis=0).astype(bf16)
+            gb = gbr[r, :, :, at].astype(f32).reshape(CH, W)
+            gp = jnp.concatenate(
+                [gb * fac[m, 256:384, :], gb * fac[m, 384:512, :]], axis=0
+            ).astype(bf16)
             gps[m, 256:512, :] = gp
-            acc_right[...] += dot(normed, gp, 1, 1)
+            acc_right[...] += dot(nrm[m], gp, 1, 1)
         return 0
 
     lax.fori_loop(0, CHUNKS, finish, 0)
     p2s[0] = blocks(acc_right[...] * INV)
     send(p2s, p2r, 0, 10)
-    sum_half(p3r, h3s, h3r, 13, 14)
-
-    def deliver_pair(m):
-        rows = pl.ds(2 * m, 2)
-        return pltpu.make_async_copy(outv.at[rows], out.at[rows], out_sem.at[m])
+    sum_both(h1s, h1r, g1s, g1r, 11, 12)
 
     def last(m, _):
-        gn = dot(w_in[...], gps[m], 1, 0) + dot(w_ig[...], gl[m], 1, 0)
-        zhat, rstd = norm_stats(mid[m].astype(f32))
+        gn = dot(w_in[...], gps[m], 1, 0) + gate[m]
+        zhat, rstd = start[m], scale[m, 0:1, :]
         acc_norm[...] += lane_sum(gn * zhat)
         gz = norm_grad(gn * cols[:, 4:5], zhat, rstd)
         res = (cott[m].astype(f32) + gz).astype(bf16)
-        outv[pl.ds(2 * m, 2)] = dot(sel[...], res, 1, 1).astype(bf16).reshape(2, RES, CH)
-        deliver_pair(m).start()
-        return 0
-
-    lax.fori_loop(0, 2 * CHUNKS, last, 0)
+        out[pl.ds(2 * m, 2)] = dot(sel[...], res, 1, 1).astype(bf16).reshape(2, RES, CH)
+        return 0
+
+    lax.fori_loop(0, CHUNKS, last, 0)
+    sum_half(p3r, h3s, h3r, 13, 14)
+    lax.fori_loop(CHUNKS, 2 * CHUNKS, last, 0)
+
+    sums[0:1, :] = jnp.sum(acc_norm[...].T, axis=0, keepdims=True)
+    g4s[...] = (sums[0:2, :] * INV).astype(bf16)
+    share(g4s, g4r, 17)
+    wait(p2r, 0, 10)
+    g2s[...] = summed(p2r.at[0], DEV).astype(bf16)
+    share(g2s, g2r, 16)
     sum_both(h3s, h3r, g3s, g3r, 14, 15)
 
-    gains = jnp.concatenate(
-        [
-            jnp.sum(acc_norm[...].T, axis=0, keepdims=True),
-            jnp.sum(acc_mid[...].T, axis=0, keepdims=True),
-            jnp.zeros((CG - 2, 128), f32),
-        ],
-        axis=0,
-    )
-    g2s[:, 256:384] = (gains * INV).astype(bf16)
-    wait(p2r, 0, 10)
-    g2s[:, 0:256] = summed(p2r.at[0], DEV).astype(bf16)
-    share(g2s, g2r, 16)
-    for m in range(2 * CHUNKS):
-        deliver_pair(m).wait()
-
-    for ident, ref in ((12, g1r), (15, g3r), (16, g2r)):
+    for ident, ref in ((12, g1r), (17, g4r), (15, g3r), (16, g2r)):
         got = ref.at[pl.ds(0, ref.shape[0] - 1)]
         pltpu.make_async_copy(got, got, recv_sem.at[ident, 0]).wait()
     o_all[0:CH, 0:256] = g3r[...].astype(f32).reshape(CH, 256)
-    o_all[0:CH, 256:512] = g2r[:, :, 0:256].astype(f32).reshape(CH, 256)
+    o_all[0:CH, 256:512] = g2r[...].astype(f32).reshape(CH, 256)
     o_all[0:CH, 512:768] = g1r[...].astype(f32).reshape(CH, 256)
-    o_all[CH : CH + CG, 0:128] = summed(g2r.at[:, :, 256:384], DEV)
+    o_all[CH : CH + 2, 0:128] = summed(g4r, DEV)
 
     for ident, ref, rest in (
         (0, b1r, (0, 1, 2)), (1, a1s, (0, 1, 2)), (2, x1s, (0, 1, 2)), (3, b2s, (0,)),
@@ -648,20 +648,31 @@
     ):
         for r in rest:
             sent(ref, r, ident)
-    for ident, ref in ((12, g1r), (15, g3r), (16, g2r)):
+    for ident, ref in ((12, g1r), (17, g4r), (15, g3r), (16, g2r)):
         gone = ref.at[pl.ds(0, ref.shape[0] - 1)]
         pltpu.make_async_copy(gone, gone, send_sem.at[ident, 0]).wait()
     across(h1s, h1r, 11).wait_send()
     across(h3s, h3r, 14).wait_send()
 
 
-def deliver(pair_in, all_in, pair_out, proj, gate, final, norm, mid):
-    pair_out[...] = pair_in[...]
-    proj[...] = all_in[0:CH, 0:512]
-    gate[...] = all_in[0:CH, 512:640]
-    final[...] = all_in[0:CH, 640:768]
+def deliver(pair_in, all_in, pair_out, proj, gate, final, norm, mid, sem):
+    copies = [
+        pltpu.make_async_copy(src, dst, sem.at[i])
+        for i, (src, dst) in enumerate(
+            (
+                (pair_in, pair_out),
+                (all_in.at[0:CH, 0:512], proj),
+                (all_in.at[0:CH, 512:640], gate),
+                (all_in.at[0:CH, 640:768], final),
+            )
+        )
+    ]
+    for copy in copies:
+        copy.start()
     norm[...] = all_in[CH : CH + 1, 0:128]
     mid[...] = all_in[CH + 1 : CH + 2, 0:128]
+    for copy in copies:
+        copy.wait()
 
 
 def shards(
@@ -676,25 +687,27 @@
     twice = v((CHUNKS, DEV, HG, LANES), bf16)
     steps = lambda dtype: v((2 * CHUNKS, CH, W), dtype)
     part, part2 = v((1, HDEV, HG, 256), bf16), v((1, DEV, CG, 256), bf16)
-    piece, piece2 = v((HG, 256), bf16), v((CG, 384), bf16)
-    full, full2 = v((HDEV, HG, 256), bf16), v((DEV, CG, 384), bf16)
+    piece, piece2, row = v((HG, 256), bf16), v((CG, 256), bf16), v((2, CH), bf16)
+    full, full2 = v((HDEV, HG, 256), bf16), v((DEV, CG, 256), bf16)
+    rows = v((DEV, 2, CH), bf16)
     square = v((CH, CH), bf16)
     block = v((ROWS, RES, CH), bf16)
     scratch = (
         [block, block] + [v((1, RES), jnp.int32)] * 2 + [v((2, CH), f32)] + [v((1, CH), f32)] * 4
         + [v((CH, 512), bf16), square, square, v((CH, 512), bf16), square, square]
-        + [pltpu.SMEM((1, RES), jnp.int32)] * 2 + [block, v((2 * CHUNKS, 4 * CH, W), bf16)]
+        + [pltpu.SMEM((1, RES), jnp.int32)] * 2 + [v((2 * CHUNKS, 4 * CH, W), bf16)]
+        + [v((2 * CHUNKS, 4 * CH, W), f32), v((2 * CHUNKS, CG, W), f32), v((CG, CH), f32)]
         + [v((W, W), bf16), v((CH, 128), f32), v((CH, 128), f32)]
         + [v((4 * CH, CH), bf16), square, square, v((4 * CH, CH), bf16), square, square]
         + [steps(f32), steps(f32), steps(bf16), steps(bf16), steps(bf16), steps(bf16)]
-        + [half] * 3 + [wire] * 6 + [part, part2, part, piece, piece2, piece, piece, piece]
-        + [twice, half, half] + [wire] * 6 + [part, part2, part, full, full2, full, piece, piece]
+        + [half] * 3 + [wire] * 6 + [part, part2, part, piece, piece2, piece, row, piece, piece]
+        + [twice, half, half] + [wire] * 6 + [part, part2, part, full, full2, full, rows, piece, piece]
         + [v((LANES // 128, DEV * HG, 128), f32), v((LANES // 128, CH, 128), f32)]
         + [v((HG, 256, 256), bf16)]
         + [v((CHUNKS, CG, RES, 128), bf16), v((CG, RES, 256), bf16), v((CHUNKS, CG, 128, 256), bf16)]
         + [v((CH, 256), f32)] * 2 + [v((CH, CH), f32)] * 4
-        + [pltpu.SemaphoreType.DMA((17, CHUNKS))] * 2
-        + [pltpu.SemaphoreType.DMA((17,)), pltpu.SemaphoreType.DMA((2 * CHUNKS,))]
+        + [pltpu.SemaphoreType.DMA((18, CHUNKS))] * 2
+        + [pltpu.SemaphoreType.DMA((17,))]
     )
     mask = residue_mask.reshape(1, RES)
     chain = chain_ids.reshape(1, RES)
@@ -712,16 +725,23 @@
     )
     got = pl.pallas_call(
         kernel,
-        out_shape=[outs[0], jax.ShapeDtypeStruct((CH + CG, 768), f32)],
+        out_shape=[pltpu.VMEM((ROWS, RES, CH), bf16), pltpu.VMEM((CH + CG, 768), f32)],
         in_specs=[hbm] * 15,
-        out_specs=[hbm, vm],
+        out_specs=[vm, vm],
         scratch_shapes=scratch,
         compiler_params=params,
     )(
         pair, cotangent, mask, chain, chain_embed, *gains,
         out_proj, out_gate, out_final, in_proj, in_gate, in_final,
     )
-    got = pl.pallas_call(deliver, out_shape=outs, in_specs=[vm] * 2, out_specs=[vm] * 6)(*got)
+    got = [pltpu.with_memory_space_constraint(g, pltpu.VMEM) for g in got]
+    got = pl.pallas_call(
+        deliver,
+        out_shape=outs,
+        in_specs=[vm] * 2,
+        out_specs=[hbm] * 4 + [vm] * 2,
+        scratch_shapes=[pltpu.SemaphoreType.DMA((4,))],
+    )(*got)
     return (*got[:4], got[4].reshape(CH), got[5].reshape(CH))
 
 

time: 136 us -> 134 us (0.985)
  Pallas kernels: 135 us -> 133 us
    pallas_call x2, Pallas kernels: 135 us -> 133 us  [the longest x1 131 us: shards(): pl.pallas_call(kernel, out_shape=[pltpu.VMEM((ROWS, RES, CH), bf16), pltp...]
where the time goes in v5:
time: 134 us
  Pallas kernels  133 us (99%)
    pallas_call x1, Pallas kernels, shards(): pl.pallas_call(kernel, out_shape=[pltpu.VMEM((ROWS, RES, CH), bf16), pltp...  131 us

profile of v5, /device:TPU:16, one launch (start us, length us, event | category | flops | bytes accessed | tf_op | source)
XLA Modules:
  0.0 133.6 jit_solution(14672827940217353925)
XLA Ops:
  0.6 131.5 %shard_map.190 = (bf16[12,192,128]{2,1,0:T(8,128)(2,1)S(1)}, f32[136,768]{1,0:T(8,128)S(1)}) custom-call(bf16[12,192,128]{2,1,0:T(8,128)(2,1)} %pair_h.1, bf16[12,192,128]{2,1,0:T(8,128)(2,1)} %cot_h.1, s32[1,192]{1,0:T(1,128)} %bitcast.8, s32[1,192]{1,0:T(1,128)} %bitcast.9, f32[2,128]{1,0:T(2,128)} %embed_h.1, f32[1,128]{1,0:T(1,128)} %bitcast.10, ...), custom_call_target="tpu_custom_call" | custom-call | tf_op jit(solution)/shard_map/pallas_call | solution.py:726
  132.1 1.5 %shard_map.191 = (bf16[12,192,128]{2,1,0:T(8,128)(2,1)}, f32[128,512]{1,0:T(8,128)}, f32[128,128]{1,0:T(8,128)}, f32[128,128]{1,0:T(8,128)}, f32[1,128]{1,0:T(1,128)}, /*index=5*/f32[1,128]{1,0:T(1,128)}) custom-call(bf16[12,192,128]{2,1,0:T(8,128)(2,1)S(1)} %get-tuple-element.14.pair_in, f32[136,768]{1,0:T(8,128)S(1)} %get-tuple-element.15.all_in), custom_call_target="tpu_custom_call" | custom-call | tf_op jit(solution)/shard_map/pallas_call | solution.py:738

commit v6 on v5

--- a/solution.py
+++ b/solution.py
@@ -267,7 +267,7 @@
             gate[m] = sig(dot(wt_og[...], normed, 1, 0))
         return 0
 
-    project(0, 0)
+    lax.fori_loop(0, 2, project, 0)
     pl.semaphore_wait(barrier, DEV - 1)
 
     def send_b1(r, _):
@@ -282,14 +282,9 @@
         blocks_out = ref.at[r, pl.ds(0, ref.shape[1] - 1)]
         pltpu.make_async_copy(blocks_out, blocks_out, send_sem.at[ident, r]).wait()
 
-    send_b1(0, 0)
-
-    def project_and_send(r, _):
-        project(r, 0)
-        send_b1(r, 0)
-        return 0
-
-    lax.fori_loop(1, CHUNKS, project_and_send, 0)
+    lax.fori_loop(0, 2, send_b1, 0)
+    project(2, 0)
+    send_b1(2, 0)
     send_a1(0, 0)
 
     for load in loads[12:]:
@@ -395,7 +390,7 @@
                     lo, res[u : u + 8, 128:256], swap(res[u + 8 : u + 16, 128:256])
                 )
 
-        channels(HG, one)
+        channels(HG, one, 16)
         flush(x1s, r)
         send_half(x1s, x1r, r, 2, HDEV - 1, near, mine)
         return 0

time: 134 us -> 133 us (level)
  no operation moved by 1% of the time
where the time goes in v6:
time: 133 us
  Pallas kernels  132 us (99%)
    pallas_call x1, Pallas kernels, shards(): pl.pallas_call(kernel, out_shape=[pltpu.VMEM((ROWS, RES, CH), bf16), pltp...  131 us

profile of v6, /device:TPU:16, one launch (start us, length us, event | category | flops | bytes accessed | tf_op | source)
XLA Modules:
  0.0 132.9 jit_solution(11189765569588825098)
XLA Ops:
  0.6 130.8 %shard_map.190 = (bf16[12,192,128]{2,1,0:T(8,128)(2,1)S(1)}, f32[136,768]{1,0:T(8,128)S(1)}) custom-call(bf16[12,192,128]{2,1,0:T(8,128)(2,1)} %pair_h.1, bf16[12,192,128]{2,1,0:T(8,128)(2,1)} %cot_h.1, s32[1,192]{1,0:T(1,128)} %bitcast.8, s32[1,192]{1,0:T(1,128)} %bitcast.9, f32[2,128]{1,0:T(2,128)} %embed_h.1, f32[1,128]{1,0:T(1,128)} %bitcast.10, ...), custom_call_target="tpu_custom_call" | custom-call | tf_op jit(solution)/shard_map/pallas_call | solution.py:721
  131.4 1.5 %shard_map.191 = (bf16[12,192,128]{2,1,0:T(8,128)(2,1)}, f32[128,512]{1,0:T(8,128)}, f32[128,128]{1,0:T(8,128)}, f32[128,128]{1,0:T(8,128)}, f32[1,128]{1,0:T(1,128)}, /*index=5*/f32[1,128]{1,0:T(1,128)}) custom-call(bf16[12,192,128]{2,1,0:T(8,128)(2,1)S(1)} %get-tuple-element.14.pair_in, f32[136,768]{1,0:T(8,128)S(1)} %get-tuple-element.15.all_in), custom_call_target="tpu_custom_call" | custom-call | tf_op jit(solution)/shard_map/pallas_call | solution.py:733
